TPU v7x, 32 devices: a whole 2x2x4 slice. The times are simulated.
32 devices in a mesh: tm: 2 (over y), lat: 4 (over x, core), lon: 4 (over z).
Axes of the slice: x: 2, y: 2, z: 4, core: 2. Of those that a mesh axis runs over, the one named last changes fastest.
Arguments:
- increments: float32 [2, 16, 32, 1536], P('tm', None, 'lat', 'lon'), may hold values from -6 to 6
- advection: float32 [16, 32, 1536], P(None, 'lat', 'lon'), may hold values from 0.2 to 0.4
- diffusion: float32 [16, 32, 1536], P(None, 'lat', 'lon'), may hold values from 0.25 to 0.3
- departures: float32 [2, 6, 16, 32, 1536], P('tm', None, None, 'lat', 'lon'), may hold values from -6 to 6
- obs_weight: float32 [16], replicated, may hold values from 0.5 to 2
- error_weight: float32 [16], replicated, may hold values from 0.5 to 2
- penalty_weight: float32 [16], replicated, may hold values from 0.5 to 2
- filter_steps: int32 [6], replicated, may hold values from 0 to 11, as said below
- filter_weights: float32 [6], replicated, may hold values from 0.05 to 0.3
Outputs:
- gradient: float32 [2, 16, 32, 1536], P('tm', None, 'lat', 'lon')
Inputs may be any that keep to these rules, and one draw needn't show every extreme that they name: filter_steps lists, for k = 0 .. 1 in turn, 3 different steps of subwindow k, each in k * 6 to k * 6 + 5.
All inputs are finite; a program needn't handle non-finite values.
Results may differ from a plain program's by a relative error of at most 0.00002.
Values sent between devices are 32-bit elements; how exact they have to be, the bound alone decides.
No kernel may reach another device: no remote copies, remote signals or barrier semaphores. Data moves between devices by JAX's collectives and lax.ppermute only.
A program may use at most 64 MiB of HBM per device.

v0:
```python
import jax
import jax.numpy as jnp
from jax import lax
from jax.sharding import PartitionSpec as P


def extended(value, sides, width):
    for axis, dim in sides:
        count, length = (lax.axis_size(axis), value.shape[dim])
        up = [(i, (i + 1) % count) for i in range(count - 1)]
        down = [(j, i) for i, j in up]
        last = lax.slice_in_dim(value, length - width, length, axis=dim)
        initial = lax.slice_in_dim(value, 0, width, axis=dim)
        before = lax.ppermute(last, axis, up)
        after = lax.ppermute(initial, axis, down)
        value = jnp.concatenate([before, value, after], axis=dim)
    return value


def passed_along(value, axis, by):
    count = lax.axis_size(axis)
    return lax.ppermute(value, axis, [(i, (i + by) % count) for i in range(count)])


def from_behind(block, axis, distance):
    devices = range(lax.axis_size(axis))
    route = [(i - distance, i) for i in devices if i - distance in devices]
    return lax.ppermute(block, axis, route)


def widen_coefficients(advection, diffusion, width):
    wide_adv, wide_dif = (
        extended(advection, (("lat", 1),), width),
        extended(diffusion, (("lat", 1),), width),
    )
    west_adv, west_dif = passed_along((wide_adv[:, :, -width:], wide_dif[:, :, -width:]), "lon", 1)
    east_adv, east_dif = passed_along((wide_adv[:, :, :width], wide_dif[:, :, :width]), "lon", -1)
    full_adv = jnp.concatenate([west_adv, wide_adv, east_adv], axis=2)
    full_dif = jnp.concatenate([west_dif, wide_dif, east_dif], axis=2)
    return (full_adv, full_dif)


def deep_forward(initial, full_adv, full_dif, inside, width):
    lat_rows = initial.shape[1]
    wide = extended(initial, (("lat", 1),), width)
    edge = passed_along(wide[:, :, -width:], "lon", 1)
    block = jnp.concatenate([edge, wide], axis=2)
    total_rows = block.shape[1]
    fore_adv = full_adv[:, :, :-width]
    fore_dif = full_dif[:, :, :-width]
    states = []
    for level in range(width):
        states.append(block[:, width - level : width - level + lat_rows, width - level :])
        adv_now = fore_adv[:, level + 1 : total_rows - level - 1, level + 1 :]
        dif_now = fore_dif[:, level + 1 : total_rows - level - 1, level + 1 :]
        centre = block[:, 1:-1, 1:]
        western = block[:, 1:-1, :-1]
        meridian = block[:, 2:, 1:] + block[:, :-2, 1:]
        fresh = (1.0 - adv_now - 2.0 * dif_now) * centre + adv_now * western + dif_now * meridian
        block = fresh * inside[level + 1 : total_rows - level - 1][None, :, None]
    return (states, block)


def deep_adjoint(start, forcings, full_adv, full_dif, inside, width):
    stacked = jnp.stack([start] + forcings)
    wide = extended(stacked, (("lat", 2),), width)
    edge = passed_along(wide[:, :, :, :width], "lon", -1)
    block_all = jnp.concatenate([wide, edge], axis=3)
    total_rows = block_all.shape[2]
    total_cols = block_all.shape[3]
    back_adv = full_adv[:, :, width:]
    back_dif = full_dif[:, :, width:]
    adjoint = block_all[0]
    for level in range(1, width + 1):
        section = width - level
        adv_now = back_adv[:, level - 1 : total_rows - level + 1, : total_cols - level + 1]
        dif_now = back_dif[:, level - 1 : total_rows - level + 1, : total_cols - level + 1]
        carried = adv_now * adjoint
        spread = dif_now * adjoint
        keep = (1.0 - adv_now - 2.0 * dif_now)[:, 1:-1, :-1]
        moved = (
            keep * adjoint[:, 1:-1, :-1]
            + carried[:, 1:-1, 1:]
            + (spread[:, 2:, :-1] + spread[:, :-2, :-1])
        )
        forcing = block_all[1 + section][:, level : total_rows - level, : total_cols - level]
        adjoint = (forcing + moved) * inside[level : total_rows - level][None, :, None]
    return adjoint


def body(
    increments,
    advection,
    diffusion,
    departures,
    obs_weight,
    error_weight,
    penalty_weight,
    filter_steps,
    filter_weights,
):
    position = lax.axis_index("tm")
    members = lax.axis_size("tm")
    count_steps = departures.shape[1]
    middle = members * count_steps // 2
    initial = increments[0]
    lat_rows = initial.shape[1]
    window_steps = position * count_steps + jnp.arange(count_steps, dtype=jnp.int32)
    hits = (filter_steps[None, :] == window_steps[:, None]).astype(jnp.float32)
    tap = jnp.sum(hits * filter_weights[None, :], axis=1)
    coef = tap - (window_steps == middle).astype(jnp.float32)
    obs_level = obs_weight[:, None, None]
    err_level = error_weight[:, None, None]
    full_adv, full_dif = widen_coefficients(advection, diffusion, count_steps)
    global_rows = (
        lax.axis_index("lat") * lat_rows
        - count_steps
        + jnp.arange(lat_rows + 2 * count_steps, dtype=jnp.int32)
    )
    inside = ((global_rows >= 0) & (global_rows < lat_rows * lax.axis_size("lat"))).astype(
        jnp.float32
    )
    states, final = deep_forward(initial, full_adv, full_dif, inside, count_steps)
    partial_value = jnp.zeros(initial.shape, jnp.float32)
    for step in range(count_steps):
        partial_value = partial_value + coef[step] * states[step]
    previous = from_behind(final, "tm", 1)
    mismatch = initial - previous
    scale = jnp.where(position == 0, jnp.ones_like(err_level), err_level)
    total = lax.psum(partial_value, "tm")
    force = penalty_weight[:, None, None] * total
    returned = from_behind(err_level * mismatch, "tm", -1)
    adjoint = -returned
    forcings = [
        obs_level * (states[step] - departures[0, step]) + coef[step] * force
        for step in range(count_steps)
    ]
    adjoint = deep_adjoint(adjoint, forcings, full_adv, full_dif, inside, count_steps)
    return (adjoint + scale * mismatch)[None]


def solution(mesh):
    return jax.shard_map(
        body,
        mesh=mesh,
        in_specs=(
            P("tm", None, "lat", "lon"),
            P(None, "lat", "lon"),
            P(None, "lat", "lon"),
            P("tm", None, None, "lat", "lon"),
            P(),
            P(),
            P(),
            P(),
            P(),
        ),
        out_specs=P("tm", None, "lat", "lon"),
        check_vma=False,
    )
```

profile of v0, /device:TPU:1, one launch (start us, length us, event | category | flops | bytes accessed | tf_op | source)
XLA Modules:
  0.0 150.3 jit_solution(9224703042511867812)
XLA Ops:
  7.6 4.5 %collective-permute-start.6 = (f32[16,6,384]{2,0,1:T(8,128)S(1)}, f32[16,6,384]{2,0,1:T(8,128)S(1)}, u32[]{:S(2)}, u32[]{:S(2)}) collective-permute-start(f32[16,6,384]{2,0,1:T(8,128)S(1)} %get-tuple-element.52), channel_id=1, source_target_pairs={{0,4},{4,8},{8,12},{1,5},{5,9},{9,13},{2,6},{6,10},{10,14},{3,7},{... | collective-permute-start | bytes 442376 | tf_op jit(solution)/shard_map/ppermute | solution.py:14
  12.1 1.9 %collective-permute-start.7 = (f32[16,6,384]{2,0,1:T(8,128)S(1)}, f32[16,6,384]{2,0,1:T(8,128)S(1)}, u32[]{:S(2)}, u32[]{:S(2)}) collective-permute-start(f32[16,6,384]{2,0,1:T(8,128)S(1)} %get-tuple-element.53), channel_id=1, source_target_pairs={{4,0},{8,4},{12,8},{5,1},{9,5},{13,9},{6,2},{10,6},{14,10},{7,3},{... | collective-permute-start | bytes 442376 | tf_op jit(solution)/shard_map/ppermute | solution.py:15
  15.2 3.6 %collective-permute-start = (f32[16,6,384]{2,0,1:T(8,128)S(1)}, f32[16,6,384]{2,0,1:T(8,128)S(1)}, u32[]{:S(2)}, u32[]{:S(2)}) collective-permute-start(f32[16,6,384]{2,0,1:T(8,128)S(1)} %copy.137), channel_id=1, source_target_pairs={{0,4},{4,8},{8,12},{1,5},{5,9},{9,13},{2,6},{6,10},{10,14},{3,7},{... | collective-permute-start | bytes 442376 | tf_op jit(solution)/shard_map/ppermute | solution.py:14
  18.9 2.1 %collective-permute-start.1 = (f32[16,6,384]{2,0,1:T(8,128)S(1)}, f32[16,6,384]{2,0,1:T(8,128)S(1)}, u32[]{:S(2)}, u32[]{:S(2)}) collective-permute-start(f32[16,6,384]{2,0,1:T(8,128)S(1)} %copy.138), channel_id=1, source_target_pairs={{4,0},{8,4},{12,8},{5,1},{9,5},{13,9},{6,2},{10,6},{14,10},{7,3},{... | collective-permute-start | bytes 442376 | tf_op jit(solution)/shard_map/ppermute | solution.py:15
  21.0 3.6 %collective-permute-start.3 = (f32[16,6,384]{2,0,1:T(8,128)S(1)}, f32[16,6,384]{2,0,1:T(8,128)S(1)}, u32[]{:S(2)}, u32[]{:S(2)}) collective-permute-start(f32[16,6,384]{2,0,1:T(8,128)S(1)} %copy.135), channel_id=1, source_target_pairs={{0,4},{4,8},{8,12},{1,5},{5,9},{9,13},{2,6},{6,10},{10,14},{3,7},{... | collective-permute-start | bytes 442376 | tf_op jit(solution)/shard_map/ppermute | solution.py:14
  26.1 1.9 %collective-permute-start.4 = (f32[16,6,384]{2,0,1:T(8,128)S(1)}, f32[16,6,384]{2,0,1:T(8,128)S(1)}, u32[]{:S(2)}, u32[]{:S(2)}) collective-permute-start(f32[16,6,384]{2,0,1:T(8,128)S(1)} %copy.136), channel_id=1, source_target_pairs={{4,0},{8,4},{12,8},{5,1},{9,5},{13,9},{6,2},{10,6},{14,10},{7,3},{... | collective-permute-start | bytes 442376 | tf_op jit(solution)/shard_map/ppermute | solution.py:15
  29.7 2.1 %collective-permute-start.14 = (f32[16,20,6]{2,0,1:T(8,128)S(1)}, f32[16,20,6]{2,0,1:T(8,128)S(1)}, u32[]{:S(2)}, u32[]{:S(2)}) collective-permute-start(f32[16,20,6]{2,0,1:T(8,128)S(1)} %get-tuple-element.44), channel_id=1, source_target_pairs={{0,3},{1,0},{2,1},{3,2},{4,7},{5,4},{6,5},{7,6},{8,11},{9,8},{10,9... | collective-permute-start | bytes 23048 | tf_op jit(solution)/shard_map/ppermute | solution.py:22
  36.2 7.1 %collective-permute-done.2 = f32[16,20,6]{2,0,1:T(8,128)S(1)} collective-permute-done((f32[16,20,6]{2,0,1:T(8,128)S(1)}, f32[16,20,6]{2,0,1:T(8,128)S(1)}, u32[]{:S(2)}, u32[]{:S(2)}) %collective-permute-start.2) | collective-permute-done | bytes 7712 | tf_op jit(solution)/shard_map/ppermute | solution.py:22
  51.8 5.0 %multiply_add_fusion = (f32[16,8,384]{2,0,1:T(8,128)}, f32[16,8,384]{2,0,1:T(8,128)S(1)}) fusion(f32[16,12,386]{2,0,1:T(8,128)S(1)} %get-tuple-element.39, f32[16,14,387]{2,0,1:T(8,128)S(1)} %get-tuple-element.41, f32[16,16,388]{2,0,1:T(8,128)S(1)} %get-tuple-element.43, f32[16,18,389]{2,0,1:T(8,128)S(1)} %fusion.9, ...), kind=kLoop, calls=%fused_computation.208 | loop fusion | flops 1032192 | bytes 2555960 | tf_op jit(solution)/shard_map/add | solution.py:126
  56.8 3.1 %collective-permute-start.9 = (f32[16,8,384]{2,0,1:T(8,128)S(1)}, f32[16,8,384]{2,0,1:T(8,128)S(1)}, u32[]{:S(2)}, u32[]{:S(2)}) collective-permute-start(f32[16,8,384]{2,0,1:T(8,128)S(1)} %get-tuple-element.49), channel_id=1, source_target_pairs={{0,16},{1,17},{2,18},{3,19},{4,20},{5,21},{6,22},{7,23},{8,24},{9,... | collective-permute-start | bytes 589832 | tf_op jit(solution)/shard_map/ppermute | solution.py:28
  59.9 4.4 %collective-permute-done.9 = f32[16,8,384]{2,0,1:T(8,128)S(1)} collective-permute-done((f32[16,8,384]{2,0,1:T(8,128)S(1)}, f32[16,8,384]{2,0,1:T(8,128)S(1)}, u32[]{:S(2)}, u32[]{:S(2)}) %collective-permute-start.9) | collective-permute-done | bytes 196640 | tf_op jit(solution)/shard_map/ppermute | solution.py:28
  66.8 6.0 %collective-permute-done.10 = f32[16,8,384]{2,0,1:T(8,128)} collective-permute-done((f32[16,8,384]{2,0,1:T(8,128)S(1)}, f32[16,8,384]{2,0,1:T(8,128)}, u32[]{:S(2)}, u32[]{:S(2)}) %collective-permute-start.10) | collective-permute-done | bytes 196640 | tf_op jit(solution)/shard_map/ppermute | solution.py:28
  73.8 15.7 %all-reduce.2.cloned.1.call-done = f32[16,8,384]{2,0,1:T(8,128)} async-done(((f32[16,8,384]{2,0,1:T(8,128)}), f32[16,8,384]{2,0,1:T(8,128)}) %all-reduce.2.cloned.1.call-update) | async-done | bytes 196624 | tf_op jit(solution)/shard_map/psum | solution.py:130
  89.5 1.9 %fusion.103 = f32[7,16,8,384]{3,1,2,0:T(8,128)S(1)} fusion(f32[7,16,8,384]{3,1,2,0:T(8,128)S(1)} %bitcast_dynamic-update-slice_fusion, f32[1,1,16,8,384]{4,3,2,1,0:T(8,128)} %get-tuple-element.35, f32[16,8,384]{2,0,1:T(8,128)} %all-reduce.2.cloned.1.call-done, f32[16]{0:T(128)S(1)} %copy-done.24, f32[]{:T(128)} %bitcast.3, f32[16]{0:T(128)S(1)} %copy-done.25, ...), kind=kLoop, calls=%fused_computation.205 | loop fusion | flops 245760 | bytes 787460
  91.4 1.9 %fusion.98 = f32[7,16,8,384]{3,1,2,0:T(8,128)S(1)} fusion(f32[7,16,8,384]{3,1,2,0:T(8,128)S(1)} %fusion.103, f32[1,1,16,8,384]{4,3,2,1,0:T(8,128)} %get-tuple-element.34, f32[16,18,389]{2,0,1:T(8,128)S(1)} %fusion.9, f32[16,8,384]{2,0,1:T(8,128)} %all-reduce.2.cloned.1.call-done, f32[]{:T(128)} %bitcast.4, f32[16]{0:T(128)S(1)} %copy-done.24, ...), kind=kLoop, calls=%fused_computation.199 | loop fusion | flops 245760 | bytes 787460
  98.9 4.1 %collective-permute-start.11 = (f32[7,16,6,384]{3,1,2,0:T(8,128)}, f32[7,16,6,384]{3,1,2,0:T(8,128)S(1)}, u32[]{:S(2)}, u32[]{:S(2)}) collective-permute-start(f32[7,16,6,384]{3,1,2,0:T(8,128)} %get-tuple-element.28), channel_id=1, source_target_pairs={{0,4},{4,8},{8,12},{1,5},{5,9},{9,13},{2,6},{6,10},{10,14},{3,7},{... | collective-permute-start | bytes 3096584 | tf_op jit(solution)/shard_map/ppermute | solution.py:14
  103.0 1.9 %collective-permute-start.12 = (f32[7,16,6,384]{3,1,2,0:T(8,128)}, f32[7,16,6,384]{3,1,2,0:T(8,128)}, u32[]{:S(2)}, u32[]{:S(2)}) collective-permute-start(f32[7,16,6,384]{3,1,2,0:T(8,128)} %get-tuple-element.29), channel_id=1, source_target_pairs={{4,0},{8,4},{12,8},{5,1},{9,5},{13,9},{6,2},{10,6},{14,10},{7,3},{... | collective-permute-start | bytes 3096584 | tf_op jit(solution)/shard_map/ppermute | solution.py:15
  105.0 9.9 %collective-permute-done.11 = f32[7,16,6,384]{3,1,2,0:T(8,128)S(1)} collective-permute-done((f32[7,16,6,384]{3,1,2,0:T(8,128)}, f32[7,16,6,384]{3,1,2,0:T(8,128)S(1)}, u32[]{:S(2)}, u32[]{:S(2)}) %collective-permute-start.11) | collective-permute-done | bytes 1032224 | tf_op jit(solution)/shard_map/ppermute | solution.py:14
  114.9 4.6 %collective-permute-done.12 = f32[7,16,6,384]{3,1,2,0:T(8,128)} collective-permute-done((f32[7,16,6,384]{3,1,2,0:T(8,128)}, f32[7,16,6,384]{3,1,2,0:T(8,128)}, u32[]{:S(2)}, u32[]{:S(2)}) %collective-permute-start.12) | collective-permute-done | bytes 1032224 | tf_op jit(solution)/shard_map/ppermute | solution.py:15
  119.5 2.1 %pad_maximum_fusion.2 = f32[7,16,20,6]{3,1,2,0:T(8,128)} fusion(f32[7,16,6,384]{3,1,2,0:T(8,128)} %collective-permute-done.12, f32[7,16,8,384]{3,1,2,0:T(8,128)S(1)} %fusion.78, f32[7,16,6,384]{3,1,2,0:T(8,128)S(1)} %collective-permute-done.11), kind=kLoop, calls=%fused_computation.20 | loop fusion | flops 26880 | bytes 3494400 | tf_op jit(solution)/shard_map/concatenate | solution.py:16
  121.6 2.9 %copy.47 = f32[7,16,20,6]{2,1,3,0:T(8,128)} copy(f32[7,16,20,6]{3,1,2,0:T(8,128)} %pad_maximum_fusion.2) | data formatting | bytes 107520 | tf_op jit(solution)/shard_map/slice | solution.py:67
  124.5 3.0 %collective-permute-start.13 = (f32[7,16,20,6]{2,1,3,0:T(8,128)}, f32[7,16,20,6]{2,1,3,0:T(8,128)S(1)}, u32[]{:S(2)}, u32[]{:S(2)}) collective-permute-start(f32[7,16,20,6]{2,1,3,0:T(8,128)} %copy.47), channel_id=1, source_target_pairs={{0,3},{1,0},{2,1},{3,2},{4,7},{5,4},{6,5},{7,6},{8,11},{9,8},{10,9... | collective-permute-start | bytes 161288 | tf_op jit(solution)/shard_map/ppermute | solution.py:22
  127.8 4.2 %collective-permute-done.13 = f32[7,16,20,6]{2,1,3,0:T(8,128)S(1)} collective-permute-done((f32[7,16,20,6]{2,1,3,0:T(8,128)}, f32[7,16,20,6]{2,1,3,0:T(8,128)S(1)}, u32[]{:S(2)}, u32[]{:S(2)}) %collective-permute-start.13) | collective-permute-done | bytes 53792 | tf_op jit(solution)/shard_map/ppermute | solution.py:22
  133.9 2.4 %pad_maximum_fusion = f32[7,16,20,390]{3,1,2,0:T(8,128)S(1)} fusion(f32[7,16,20,6]{3,1,2,0:T(8,128)} %copy.48, f32[7,16,6,384]{3,1,2,0:T(8,128)} %collective-permute-done.12, f32[7,16,8,384]{3,1,2,0:T(8,128)S(1)} %fusion.78, f32[7,16,6,384]{3,1,2,0:T(8,128)} %copy-done.8), kind=kLoop, calls=%fused_computation | loop fusion | flops 2620800 | bytes 6988800 | tf_op jit(solution)/shard_map/concatenate | solution.py:68
  (128 shorter events, 36.1 us)
Async XLA Ops:
  6.5 14.4 %copy-start.13 = (f32[16,8,384]{2,1,0:T(8,128)S(1)}, f32[16,8,384]{2,1,0:T(8,128)}, u32[]{:S(2)}) copy-start(f32[16,8,384]{2,1,0:T(8,128)} %param.11) | copy-start | bytes 589828
  6.5 82.9 %all-reduce.2.cloned.1.call-start = ((), (), s32[]{:S(2)}) async-start(), calls=%async_computation | async-start | bytes 393216 | tf_op jit(solution)/shard_map/psum | solution.py:130
  7.6 17.1 %copy-start.26 = (f32[6]{0:T(128)S(1)}, f32[6]{0:T(128)}, u32[]{:S(2)}) copy-start(f32[6]{0:T(128)} %param.17) | copy-start | bytes 76
  7.6 17.1 %copy-start.27 = (s32[6]{0:T(128)S(1)}, s32[6]{0:T(128)}, u32[]{:S(2)}) copy-start(s32[6]{0:T(128)} %param.16) | copy-start | bytes 76
  7.6 18.4 %collective-permute-start.6 = (f32[16,6,384]{2,0,1:T(8,128)S(1)}, f32[16,6,384]{2,0,1:T(8,128)S(1)}, u32[]{:S(2)}, u32[]{:S(2)}) collective-permute-start(f32[16,6,384]{2,0,1:T(8,128)S(1)} %get-tuple-element.52), channel_id=1, source_target_pairs={{0,4},{4,8},{8,12},{1,5},{5,9},{9,13},{2,6},{6,10},{10,14},{3,7},{... | collective-permute-start | bytes 442376 | tf_op jit(solution)/shard_map/ppermute | solution.py:14
  12.1 15.9 %collective-permute-start.7 = (f32[16,6,384]{2,0,1:T(8,128)S(1)}, f32[16,6,384]{2,0,1:T(8,128)S(1)}, u32[]{:S(2)}, u32[]{:S(2)}) collective-permute-start(f32[16,6,384]{2,0,1:T(8,128)S(1)} %get-tuple-element.53), channel_id=1, source_target_pairs={{4,0},{8,4},{12,8},{5,1},{9,5},{13,9},{6,2},{10,6},{14,10},{7,3},{... | collective-permute-start | bytes 442376 | tf_op jit(solution)/shard_map/ppermute | solution.py:15
  15.2 14.3 %collective-permute-start = (f32[16,6,384]{2,0,1:T(8,128)S(1)}, f32[16,6,384]{2,0,1:T(8,128)S(1)}, u32[]{:S(2)}, u32[]{:S(2)}) collective-permute-start(f32[16,6,384]{2,0,1:T(8,128)S(1)} %copy.137), channel_id=1, source_target_pairs={{0,4},{4,8},{8,12},{1,5},{5,9},{9,13},{2,6},{6,10},{10,14},{3,7},{... | collective-permute-start | bytes 442376 | tf_op jit(solution)/shard_map/ppermute | solution.py:14
  18.9 10.7 %collective-permute-start.1 = (f32[16,6,384]{2,0,1:T(8,128)S(1)}, f32[16,6,384]{2,0,1:T(8,128)S(1)}, u32[]{:S(2)}, u32[]{:S(2)}) collective-permute-start(f32[16,6,384]{2,0,1:T(8,128)S(1)} %copy.138), channel_id=1, source_target_pairs={{4,0},{8,4},{12,8},{5,1},{9,5},{13,9},{6,2},{10,6},{14,10},{7,3},{... | collective-permute-start | bytes 442376 | tf_op jit(solution)/shard_map/ppermute | solution.py:15
  21.0 10.8 %collective-permute-start.3 = (f32[16,6,384]{2,0,1:T(8,128)S(1)}, f32[16,6,384]{2,0,1:T(8,128)S(1)}, u32[]{:S(2)}, u32[]{:S(2)}) collective-permute-start(f32[16,6,384]{2,0,1:T(8,128)S(1)} %copy.135), channel_id=1, source_target_pairs={{0,4},{4,8},{8,12},{1,5},{5,9},{9,13},{2,6},{6,10},{10,14},{3,7},{... | collective-permute-start | bytes 442376 | tf_op jit(solution)/shard_map/ppermute | solution.py:14
  26.1 6.8 %collective-permute-start.4 = (f32[16,6,384]{2,0,1:T(8,128)S(1)}, f32[16,6,384]{2,0,1:T(8,128)S(1)}, u32[]{:S(2)}, u32[]{:S(2)}) collective-permute-start(f32[16,6,384]{2,0,1:T(8,128)S(1)} %copy.136), channel_id=1, source_target_pairs={{4,0},{8,4},{12,8},{5,1},{9,5},{13,9},{6,2},{10,6},{14,10},{7,3},{... | collective-permute-start | bytes 442376 | tf_op jit(solution)/shard_map/ppermute | solution.py:15
  28.1 7.8 %collective-permute-start.8 = (f32[16,20,6]{2,0,1:T(8,128)S(1)}, f32[16,20,6]{2,0,1:T(8,128)S(1)}, u32[]{:S(2)}, u32[]{:S(2)}) collective-permute-start(f32[16,20,6]{2,0,1:T(8,128)S(1)} %pad_maximum_fusion.7), channel_id=1, source_target_pairs={{0,1},{1,2},{2,3},{3,0},{4,5},{5,6},{6,7},{7,4},{8,9},{9,10},{10,1... | collective-permute-start | bytes 23048 | tf_op jit(solution)/shard_map/ppermute | solution.py:22
  29.7 16.3 %collective-permute-start.14 = (f32[16,20,6]{2,0,1:T(8,128)S(1)}, f32[16,20,6]{2,0,1:T(8,128)S(1)}, u32[]{:S(2)}, u32[]{:S(2)}) collective-permute-start(f32[16,20,6]{2,0,1:T(8,128)S(1)} %get-tuple-element.44), channel_id=1, source_target_pairs={{0,3},{1,0},{2,1},{3,2},{4,7},{5,4},{6,5},{7,6},{8,11},{9,8},{10,9... | collective-permute-start | bytes 23048 | tf_op jit(solution)/shard_map/ppermute | solution.py:22
  31.8 11.5 %collective-permute-start.2 = (f32[16,20,6]{2,0,1:T(8,128)S(1)}, f32[16,20,6]{2,0,1:T(8,128)S(1)}, u32[]{:S(2)}, u32[]{:S(2)}) collective-permute-start(f32[16,20,6]{2,0,1:T(8,128)S(1)} %get-tuple-element.45), channel_id=1, source_target_pairs={{0,1},{1,2},{2,3},{3,0},{4,5},{5,6},{6,7},{7,4},{8,9},{9,10},{10,1... | collective-permute-start | bytes 23048 | tf_op jit(solution)/shard_map/ppermute | solution.py:22
  33.5 11.5 %collective-permute-start.5 = (f32[16,20,6]{2,0,1:T(8,128)S(1)}, f32[16,20,6]{2,0,1:T(8,128)S(1)}, u32[]{:S(2)}, u32[]{:S(2)}) collective-permute-start(f32[16,20,6]{2,0,1:T(8,128)S(1)} %get-tuple-element.46), channel_id=1, source_target_pairs={{0,1},{1,2},{2,3},{3,0},{4,5},{5,6},{6,7},{7,4},{8,9},{9,10},{10,1... | collective-permute-start | bytes 23048 | tf_op jit(solution)/shard_map/ppermute | solution.py:22
  51.7 12.7 %copy-start.4 = (f32[16,10,385]{2,0,1:T(8,128)}, f32[16,10,385]{2,0,1:T(8,128)S(1)}, u32[]{:S(2)}) copy-start(f32[16,10,385]{2,0,1:T(8,128)S(1)} %get-tuple-element.37) | copy-start | bytes 739204
  51.8 14.0 %copy-start.17 = (f32[1,6,16,8,384]{4,3,2,1,0:T(8,128)S(1)}, f32[1,6,16,8,384]{4,3,2,1,0:T(8,128)}, u32[]{:S(2)}) copy-start(f32[1,6,16,8,384]{4,3,2,1,0:T(8,128)} %param.12) | copy-start | bytes 3538948
  56.8 7.5 %collective-permute-start.9 = (f32[16,8,384]{2,0,1:T(8,128)S(1)}, f32[16,8,384]{2,0,1:T(8,128)S(1)}, u32[]{:S(2)}, u32[]{:S(2)}) collective-permute-start(f32[16,8,384]{2,0,1:T(8,128)S(1)} %get-tuple-element.49), channel_id=1, source_target_pairs={{0,16},{1,17},{2,18},{3,19},{4,20},{5,21},{6,22},{7,23},{8,24},{9,... | collective-permute-start | bytes 589832 | tf_op jit(solution)/shard_map/ppermute | solution.py:28
  64.4 25.1 %copy-start.24 = (f32[16]{0:T(128)S(1)}, f32[16]{0:T(128)}, u32[]{:S(2)}) copy-start(f32[16]{0:T(128)} %param.15) | copy-start | bytes 196
  64.4 25.1 %copy-start.25 = (f32[16]{0:T(128)S(1)}, f32[16]{0:T(128)}, u32[]{:S(2)}) copy-start(f32[16]{0:T(128)} %param.13) | copy-start | bytes 196
  64.5 8.4 %collective-permute-start.10 = (f32[16,8,384]{2,0,1:T(8,128)S(1)}, f32[16,8,384]{2,0,1:T(8,128)}, u32[]{:S(2)}, u32[]{:S(2)}) collective-permute-start(f32[16,8,384]{2,0,1:T(8,128)S(1)} %broadcast_multiply_fusion), channel_id=1, source_target_pairs={{16,0},{17,1},{18,2},{19,3},{20,4},{21,5},{22,6},{23,7},{24,8},{25... | collective-permute-start | bytes 589832 | tf_op jit(solution)/shard_map/ppermute | solution.py:28
  98.9 16.0 %collective-permute-start.11 = (f32[7,16,6,384]{3,1,2,0:T(8,128)}, f32[7,16,6,384]{3,1,2,0:T(8,128)S(1)}, u32[]{:S(2)}, u32[]{:S(2)}) collective-permute-start(f32[7,16,6,384]{3,1,2,0:T(8,128)} %get-tuple-element.28), channel_id=1, source_target_pairs={{0,4},{4,8},{8,12},{1,5},{5,9},{9,13},{2,6},{6,10},{10,14},{3,7},{... | collective-permute-start | bytes 3096584 | tf_op jit(solution)/shard_map/ppermute | solution.py:14
  103.0 16.4 %collective-permute-start.12 = (f32[7,16,6,384]{3,1,2,0:T(8,128)}, f32[7,16,6,384]{3,1,2,0:T(8,128)}, u32[]{:S(2)}, u32[]{:S(2)}) collective-permute-start(f32[7,16,6,384]{3,1,2,0:T(8,128)} %get-tuple-element.29), channel_id=1, source_target_pairs={{4,0},{8,4},{12,8},{5,1},{9,5},{13,9},{6,2},{10,6},{14,10},{7,3},{... | collective-permute-start | bytes 3096584 | tf_op jit(solution)/shard_map/ppermute | solution.py:15
  124.5 7.6 %collective-permute-start.13 = (f32[7,16,20,6]{2,1,3,0:T(8,128)}, f32[7,16,20,6]{2,1,3,0:T(8,128)S(1)}, u32[]{:S(2)}, u32[]{:S(2)}) collective-permute-start(f32[7,16,20,6]{2,1,3,0:T(8,128)} %copy.47), channel_id=1, source_target_pairs={{0,3},{1,0},{2,1},{3,2},{4,7},{5,4},{6,5},{7,6},{8,11},{9,8},{10,9... | collective-permute-start | bytes 161288 | tf_op jit(solution)/shard_map/ppermute | solution.py:22
  127.5 9.3 %collective-permute-start.15 = (f32[16,20,6]{2,0,1:T(8,128)}, f32[16,20,6]{2,0,1:T(8,128)S(1)}, u32[]{:S(2)}, u32[]{:S(2)}) collective-permute-start(f32[16,20,6]{2,0,1:T(8,128)} %get-tuple-element.47), channel_id=1, source_target_pairs={{0,3},{1,0},{2,1},{3,2},{4,7},{5,4},{6,5},{7,6},{8,11},{9,8},{10,9... | collective-permute-start | bytes 23048 | tf_op jit(solution)/shard_map/ppermute | solution.py:22
  (22 other events, 77.1 us)
Sparse Core Ops, SparseCore 0:
  66.9 22.4 all-reduce.1
where the time goes:
time: 151 us; the launch traced here: 150 us
  waiting for transfers between devices  55.8 us (37%)
  starting transfers between devices  36.2 us (24%)
  other arithmetic  27.9 us (18%)
  local copies, waits for them, and re-layouts  16.3 us (11%)
  between operations  14 us (9%)
    ppermute x4, starting transfers between devices, extended(): before = lax.ppermute(last, axis, up)  15.9 us
    psum x1, waiting for transfers between devices, body(): total = lax.psum(partial_value, 'tm')  15.7 us
    ppermute x6, waiting for transfers between devices, passed_along(): lax.ppermute(value, axis, [(i, (i + by) % count) for i in range(count)])  14.2 us
    ppermute x2, waiting for transfers between devices, from_behind(): return lax.ppermute(block, axis, route)  10.4 us
    ppermute x4, waiting for transfers between devices, extended(): before = lax.ppermute(last, axis, up)  9.93 us
    ppermute x6, starting transfers between devices, passed_along(): lax.ppermute(value, axis, [(i, (i + by) % count) for i in range(count)])  8.06 us
    unnamed x6, other arithmetic  7.99 us
    ppermute x4, starting transfers between devices, extended(): after = lax.ppermute(initial, axis, down)  7.81 us
  transfers between devices with their start and end apart: 17, of which 10 were waited for; matrix products, arithmetic and copies ran while one was open for 8% of the time, Pallas kernels for 0%

commit v1 on v0

v1 whole, which is shorter than its diff:
```python
import functools
import jax
import jax.numpy as jnp
from jax import lax
from jax.experimental import pallas as pl
from jax.experimental.pallas import tpu as pltpu
from jax.sharding import PartitionSpec as P

LANES = 128
F32 = jnp.float32
VM = pl.BlockSpec(memory_space=pltpu.VMEM)
SM = pl.BlockSpec(memory_space=pltpu.SMEM)


def call(kernel, operands, specs, shapes, scratch=(), name=None):
    return pl.pallas_call(
        kernel,
        out_shape=[jax.ShapeDtypeStruct(s, F32) for s in shapes],
        in_specs=specs,
        out_specs=[VM] * len(shapes),
        scratch_shapes=list(scratch),
        name=name,
    )(*operands)


def slot_width(steps):
    width = 8
    while width < steps:
        width *= 2
    return width


def lane_slots(count, steps):
    per_tile = LANES // slot_width(steps)
    return -(-count // per_tile)


def pack_slots(tiles, levels, steps, first_lane):
    width = slot_width(steps)
    per_tile = LANES // width
    lane = lax.broadcasted_iota(jnp.int32, (levels, LANES), 1)
    packed = []
    for base in range(0, len(tiles), per_tile):
        acc = jnp.zeros((levels, LANES), F32)
        for slot, tile in enumerate(tiles[base : base + per_tile]):
            moved = pltpu.roll(tile(), (slot * width - first_lane) % LANES, 1)
            acc = jnp.where((lane >= slot * width) & (lane < slot * width + steps), moved, acc)
        packed.append(acc)
    return packed


def unpack_slot(packed_ref, index, levels, steps, first_lane):
    width = slot_width(steps)
    per_tile = LANES // width
    base, slot = divmod(index, per_tile)
    lane = lax.broadcasted_iota(jnp.int32, (levels, LANES), 1)
    tile = packed_ref[:, base * LANES : (base + 1) * LANES]
    moved = pltpu.roll(tile, (first_lane - slot * width) % LANES, 1)
    return jnp.where((lane >= first_lane) & (lane < first_lane + steps), moved, 0.0)


def read_row(ref, levels, rows, r, base=0):
    tiles = ref.shape[0] // (levels * rows) if not base else base[1]
    start = base[0] * levels * rows * tiles if base else 0
    return jnp.concatenate(
        [ref[pl.ds(start + c * rows + r, levels, stride=rows * tiles), :] for c in range(tiles)], axis=1
    )


def tiled(block):
    *lead, rows, cols = block.shape
    split = block.reshape((*lead, rows, cols // LANES, LANES))
    return jnp.swapaxes(split, -3, -2).reshape((-1, LANES))


def untiled(flat, levels, rows, cols):
    split = flat.reshape((levels, cols // LANES, rows, LANES))
    return jnp.swapaxes(split, 1, 2).reshape((levels, rows, cols))


def pack_kernel(steps, rows, levels, x_ref, adv_ref, dif_ref, own_ref, up_ref, down_ref):
    halos = (steps, steps - 1, steps - 1)
    base = 0
    for field, ref in enumerate((x_ref, adv_ref, dif_ref)):
        halo = halos[field]
        for r in range(rows):
            value = read_row(ref, levels, rows, r)
            own_ref[field, r] = value
            if r < halo:
                down_ref[base + r] = value
            if r >= rows - halo:
                up_ref[base + r - (rows - halo)] = value
        base += halo


def row_source(steps, rows, field, row, own_ref, before_ref, after_ref):
    halo = (steps, steps - 1, steps - 1)[field]
    base = (0, steps, 2 * steps - 1)[field]
    if row < 0:
        return before_ref, (base + row + halo,)
    if row >= rows:
        return after_ref, (base + row - rows,)
    return own_ref, (field, row)


def wide_rows(steps, rows):
    listed = [(0, r) for r in range(-steps, rows + steps)]
    for field in (1, 2):
        listed += [(field, r) for r in range(-(steps - 1), rows + steps - 1)]
    return listed


def strip_kernel(steps, rows, levels, own_ref, before_ref, after_ref, out_ref):
    def tile(field, row):
        ref, index = row_source(steps, rows, field, row, own_ref, before_ref, after_ref)
        return lambda: ref[index + (slice(None), slice(-LANES, None))]

    packed = pack_slots(
        [tile(f, r) for f, r in wide_rows(steps, rows)], levels, steps, LANES - steps
    )
    for i, value in enumerate(packed):
        out_ref[:, i * LANES : (i + 1) * LANES] = value


def coefficients(position, middle, steps, taps_ref, weights_ref):
    found = []
    for s in range(steps):
        step = position * steps + s
        total = jnp.where(step == middle, -1.0, 0.0).astype(F32)
        for j in range(taps_ref.shape[0]):
            total = total + jnp.where(taps_ref[j] == step, weights_ref[j], 0.0)
        found.append(total)
    return found


def forward_kernel(
    steps, rows, levels, middle,
    position_ref, taps_ref, weights_ref, obs_ref, own_ref, before_ref, after_ref, strip_ref, dep_ref,
    adv_ref, dif_ref, keep_ref, forcing_ref, filt_ref, final_ref,
    a_ref, b_ref,
):
    cols = own_ref.shape[-1]
    wide = cols + LANES
    coef = coefficients(position_ref[0], middle, steps, taps_ref, weights_ref)
    obs = jnp.broadcast_to(obs_ref[...], (levels, cols))
    targets = (a_ref, adv_ref, dif_ref)
    for index, (field, row) in enumerate(wide_rows(steps, rows)):
        ref, where = row_source(steps, rows, field, row, own_ref, before_ref, after_ref)
        target = targets[field]
        target[row + steps, :, :LANES] = unpack_slot(strip_ref, index, levels, steps, LANES - steps)
        target[row + steps, :, LANES:] = ref[where]
    for ref in (adv_ref, dif_ref):
        for row in (0, rows + 2 * steps - 1):
            ref[row] = jnp.zeros((levels, wide), F32)
    for row in range(rows + 2 * steps):
        keep_ref[row] = 1.0 - adv_ref[row] - 2.0 * dif_ref[row]
    current, fresh = a_ref, b_ref
    for s in range(steps):
        for r in range(rows):
            state = current[r + steps, :, LANES:]
            departure = read_row(dep_ref, levels, rows, r, (s, cols // LANES))
            forcing_ref[s, r] = obs * (state - departure)
            if s == 0:
                filt_ref[r] = coef[s] * state
            else:
                filt_ref[r] = filt_ref[r] + coef[s] * state
        for row in range(s + 1, rows + 2 * steps - s - 1):
            here = current[row]
            western = pltpu.roll(here, 1, 1)
            meridian = current[row + 1] + current[row - 1]
            fresh[row] = keep_ref[row] * here + adv_ref[row] * western + dif_ref[row] * meridian
        current, fresh = fresh, current
    for r in range(rows):
        final_ref[r] = current[r + steps, :, LANES:]


def adjoint_kernel(
    steps, rows, levels, middle, members,
    position_ref, taps_ref, weights_ref, err_ref, pen_ref,
    adv_ref, dif_ref, keep_ref, forcing_ref, filt_ref, other_ref, final_ref, next_ref,
    main_ref, strip_ref,
    a_ref, b_ref, force_ref,
):
    cols = forcing_ref.shape[-1]
    wide = cols + LANES
    total_rows = rows + 2 * steps
    position = position_ref[0]
    coef = coefficients(position, middle, steps, taps_ref, weights_ref)
    linked = jnp.where(position == members - 1, 0.0, 1.0).astype(F32)
    err = jnp.broadcast_to(err_ref[...], (levels, cols)) * linked
    pen = jnp.broadcast_to(pen_ref[...], (levels, cols))
    zero = jnp.zeros((levels, wide), F32)
    for row in range(total_rows):
        if row < steps or row >= rows + steps:
            a_ref[row] = zero
            b_ref[row] = zero
    for r in range(rows):
        following = read_row(next_ref, levels, rows, r)
        a_ref[r + steps, :, :LANES] = zero[:, :LANES]
        a_ref[r + steps, :, LANES:] = err * (final_ref[r] - following)
        force_ref[r] = pen * (filt_ref[r] + other_ref[r])
    current, fresh = a_ref, b_ref
    for j in range(steps):
        s = steps - 1 - j
        for row in range(steps - j - 1, rows + steps + j + 1):
            here = current[row]
            value = keep_ref[row] * here + pltpu.roll(adv_ref[row] * here, wide - 1, 1)
            if row + 1 < total_rows:
                value = value + dif_ref[row + 1] * current[row + 1]
            if row >= 1:
                value = value + dif_ref[row - 1] * current[row - 1]
            r = row - steps
            if 0 <= r < rows:
                fresh[row, :, :LANES] = value[:, :LANES]
                fresh[row, :, LANES:] = value[:, LANES:] + (forcing_ref[s, r] + coef[s] * force_ref[r])
            else:
                fresh[row] = value
        current, fresh = fresh, current
    for row in range(total_rows):
        main_ref[row] = current[row, :, LANES:]
    packed = pack_slots(
        [functools.partial(lambda q: current[q, :, :LANES], row) for row in range(total_rows)],
        levels, steps, LANES - steps,
    )
    for i, value in enumerate(packed):
        strip_ref[:, i * LANES : (i + 1) * LANES] = value


def spill_kernel(steps, rows, levels, main_ref, strip_ref, up_ref, down_ref):
    for i in range(steps):
        for ref, row in ((down_ref, i), (up_ref, rows + steps + i)):
            ref[i, :, :-LANES] = main_ref[row, :, :-LANES]
            ref[i, :, -LANES:] = main_ref[row, :, -LANES:] + unpack_slot(
                strip_ref, row, levels, steps, LANES - steps
            )


def final_kernel(
    steps, rows, levels,
    position_ref, err_ref, main_ref, strip_ref, before_ref, after_ref, x_ref, previous_ref, out_ref,
):
    cols = main_ref.shape[-1]
    err = jnp.broadcast_to(err_ref[...], (levels, cols))
    scale = jnp.where(position_ref[0] == 0, jnp.ones_like(err), err)
    for r in range(rows):
        row = r + steps
        spilled = unpack_slot(strip_ref, row, levels, steps, LANES - steps)
        value = jnp.concatenate(
            [main_ref[row, :, :-LANES], main_ref[row, :, -LANES:] + spilled], axis=1
        )
        if r < steps:
            value = value + before_ref[r]
        if r >= rows - steps:
            value = value + after_ref[r - (rows - steps)]
        value = value + scale * (x_ref[r] - previous_ref[r])
        tiles = cols // LANES
        for c in range(tiles):
            out_ref[pl.ds(c * rows + r, levels, stride=rows * tiles), :] = value[:, c * LANES : (c + 1) * LANES]


def along(value, axis, by, ring=False):
    count = lax.axis_size(axis)
    if ring:
        return lax.ppermute(value, axis, [(i, (i + by) % count) for i in range(count)])
    return lax.ppermute(value, axis, [(i, i + by) for i in range(count) if 0 <= i + by < count])


def halves(value, axis):
    count = lax.axis_size(axis)
    if count & (count - 1):
        return lax.psum(value, axis), jnp.zeros_like(value)
    distance = 1
    other = jnp.zeros_like(value)
    while distance < count:
        if distance > 1:
            value = value + other
        other = lax.ppermute(value, axis, [(i, i ^ distance) for i in range(count)])
        distance *= 2
    return value, other


def body(
    increments, advection, diffusion, departures,
    obs_weight, error_weight, penalty_weight, filter_steps, filter_weights,
):
    members = lax.axis_size("tm")
    _, steps, levels, rows, cols = departures.shape
    middle = members * steps // 2
    position = lax.axis_index("tm").astype(jnp.int32)[None]
    obs, err, pen = (w[:, None] for w in (obs_weight, error_weight, penalty_weight))
    x, adv, dif, dep = (tiled(v) for v in (increments, advection, diffusion, departures))
    bind = functools.partial
    total_rows = rows + 2 * steps
    wide = cols + LANES
    halo_rows = 3 * steps - 2
    row_set = (levels, cols)

    own, up, down = call(
        bind(pack_kernel, steps, rows, levels), (x, adv, dif), [VM] * 3,
        [(3, rows) + row_set, (halo_rows,) + row_set, (halo_rows,) + row_set], name="pack",
    )
    before = along(up, "lat", 1)
    after = along(down, "lat", -1)
    following = along(x, "tm", -1)

    strip_shape = (levels, LANES * lane_slots(len(wide_rows(steps, rows)), steps))
    (strip,) = call(
        bind(strip_kernel, steps, rows, levels), (own, before, after), [VM] * 3, [strip_shape], name="strip",
    )
    strip = along(strip, "lon", 1, ring=True)

    wide_shape = (total_rows, levels, wide)
    adv_w, dif_w, keep_w, forcing, filt, final = call(
        bind(forward_kernel, steps, rows, levels, middle),
        (position, filter_steps, filter_weights, obs, own, before, after, strip, dep),
        [SM] * 3 + [VM] * 6,
        [wide_shape] * 3 + [(steps, rows) + row_set, (rows,) + row_set, (rows,) + row_set],
        [pltpu.VMEM(wide_shape, F32)] * 2, name="forward",
    )
    filt, other = halves(filt, "tm")
    previous = along(final, "tm", 1)

    main, spill = call(
        bind(adjoint_kernel, steps, rows, levels, middle, members),
        (position, filter_steps, filter_weights, err, pen, adv_w, dif_w, keep_w, forcing, filt, other, final, following),
        [SM] * 3 + [VM] * 10,
        [(total_rows,) + row_set, (levels, LANES * lane_slots(total_rows, steps))],
        [pltpu.VMEM(wide_shape, F32)] * 2 + [pltpu.VMEM((rows,) + row_set, F32)], name="adjoint",
    )
    spill = along(spill, "lon", -1, ring=True)
    up, down = call(
        bind(spill_kernel, steps, rows, levels), (main, spill), [VM] * 2, [(steps,) + row_set] * 2, name="spill",
    )
    before = along(up, "lat", 1)
    after = along(down, "lat", -1)
    (out,) = call(
        bind(final_kernel, steps, rows, levels),
        (position, err, main, spill, before, after, own[0], previous), [SM] + [VM] * 7, [x.shape], name="final",
    )
    return untiled(out, levels, rows, cols)[None]


def solution(mesh):
    return jax.shard_map(
        body,
        mesh=mesh,
        in_specs=(
            P("tm", None, "lat", "lon"),
            P(None, "lat", "lon"),
            P(None, "lat", "lon"),
            P("tm", None, None, "lat", "lon"),
            P(),
            P(),
            P(),
            P(),
            P(),
        ),
        out_specs=P("tm", None, "lat", "lon"),
        check_vma=False,
    )
```

time: 151 us -> 60.5 us (0.40)
  waiting for transfers between devices: 55.8 us -> 14.2 us
  other arithmetic: 27.9 us -> 0 us
  Pallas kernels: 0 us -> 17.4 us
  starting transfers between devices: 36.2 us -> 21.4 us
  between operations: 14 us -> 0.11 us
  local copies, waits for them, and re-layouts: 16.3 us -> 6.98 us
    ppermute x16 -> x9, waiting for transfers between devices: 40.1 us -> 14.2 us  [the longest x6 10.5 us: along(): lax.ppermute(value, axis, [(i, i + by) for i in range(count) if 0 <= i +...]
    pallas_call x0 -> x6, Pallas kernels: none -> 17.4 us  [call(): pl.pallas_call(kernel, out_shape=[jax.ShapeDtypeStruct(s, F32) for s in s...]
    psum x1 -> x0, waiting for transfers between devices: 15.7 us -> none  [body(): total = lax.psum(partial_value, 'tm')]
    ppermute x16 -> x9, starting transfers between devices: 36.2 us -> 21.4 us  [the longest x6 17.4 us: along(): lax.ppermute(value, axis, [(i, i + by) for i in range(count) if 0 <= i +...]
    concatenate x8 -> x0, other arithmetic: 10.6 us -> none  [the longest x4 5.72 us: widen_coefficients(): full_adv = jnp.concatenate([west_adv, wide_adv, east_adv], axis=2)]
    slice x15 -> x0, local copies, waits for them, and re-layouts: 8.43 us -> none  [the longest x1 2.85 us: deep_adjoint(): edge = passed_along(wide[:, :, :, :width], 'lon', -1)]
    unnamed x6 -> x0, other arithmetic: 7.99 us -> none
    add x2 -> x0, other arithmetic: 5.02 us -> none  [the longest x1 5.02 us: body(): partial_value = partial_value + coef[step] * states[step]]
  transfers between devices with their start and end apart: 17 -> 9, of which waited for: 10 -> 5; matrix products, arithmetic and copies ran while one was open for 8% -> 6% of each run, Pallas kernels for 0% -> 11%
where the time goes in v1:
time: 60.5 us; the launch traced here: 60.1 us
  starting transfers between devices  21.4 us (35%)
  Pallas kernels  17.4 us (29%)
  waiting for transfers between devices  14.2 us (23%)
  local copies, waits for them, and re-layouts  6.98 us (12%)
    ppermute x6, starting transfers between devices, along(): lax.ppermute(value, axis, [(i, i + by) for i in range(count) if 0 <= i +...  17.4 us
    pallas_call x6, Pallas kernels, call(): pl.pallas_call(kernel, out_shape=[jax.ShapeDtypeStruct(s, F32) for s in s...  17.4 us
    ppermute x6, waiting for transfers between devices, along(): lax.ppermute(value, axis, [(i, i + by) for i in range(count) if 0 <= i +...  10.5 us
    unnamed x28, local copies, waits for them, and re-layouts  3.35 us
    ppermute x2, starting transfers between devices, along(): lax.ppermute(value, axis, [(i, (i + by) % count) for i in range(count)])  2.76 us
    ppermute x1, waiting for transfers between devices, halves(): other = lax.ppermute(value, axis, [(i, i ^ distance) for i in range(count)])  2.14 us
    broadcast_in_dim x3, local copies, waits for them, and re-layouts, body(): w[:, None]  2.02 us
    squeeze x1, local copies, waits for them, and re-layouts, body(): own[0]  1.61 us
  transfers between devices with their start and end apart: 9, of which 5 were waited for; matrix products, arithmetic and copies ran while one was open for 6% of the time, Pallas kernels for 11%

profile of v1, /device:TPU:1, one launch (start us, length us, event | category | flops | bytes accessed | tf_op | source)
XLA Modules:
  0.0 60.1 jit_solution(13684323931024278114)
XLA Ops:
  0.0 2.4 %pack.1 = (f32[3,8,16,384]{3,2,1,0:T(8,128)}, f32[16,16,384]{2,1,0:T(8,128)}, f32[16,16,384]{2,1,0:T(8,128)}) custom-call(f32[384,128]{1,0:T(8,128)} %bitcast.34, f32[384,128]{1,0:T(8,128)} %bitcast.32, f32[384,128]{1,0:T(8,128)} %bitcast.33), custom_call_target="tpu_custom_call" | custom-call | tf_op jit(solution)/shard_map/pack/pallas_call | solution.py:16
  2.4 4.5 %collective-permute-start = (f32[16,16,384]{2,1,0:T(8,128)}, f32[16,16,384]{2,1,0:T(8,128)S(1)}, u32[]{:S(2)}, u32[]{:S(2)}) collective-permute-start(f32[16,16,384]{2,1,0:T(8,128)} %get-tuple-element.19), channel_id=1, source_target_pairs={{0,4},{4,8},{8,12},{1,5},{5,9},{9,13},{2,6},{6,10},{10,14},{3,7},{... | collective-permute-start | bytes 1179656 | tf_op jit(solution)/shard_map/ppermute | solution.py:265
  6.9 1.9 %collective-permute-start.1 = (f32[16,16,384]{2,1,0:T(8,128)}, f32[16,16,384]{2,1,0:T(8,128)S(1)}, u32[]{:S(2)}, u32[]{:S(2)}) collective-permute-start(f32[16,16,384]{2,1,0:T(8,128)} %get-tuple-element.20), channel_id=1, source_target_pairs={{4,0},{8,4},{12,8},{5,1},{9,5},{13,9},{6,2},{10,6},{14,10},{7,3},{... | collective-permute-start | bytes 1179656 | tf_op jit(solution)/shard_map/ppermute | solution.py:265
  8.8 3.1 %collective-permute-done.before_ref = f32[16,16,384]{2,1,0:T(8,128)S(1)} collective-permute-done((f32[16,16,384]{2,1,0:T(8,128)}, f32[16,16,384]{2,1,0:T(8,128)S(1)}, u32[]{:S(2)}, u32[]{:S(2)}) %collective-permute-start) | collective-permute-done | bytes 393248 | tf_op jit(solution)/shard_map/ppermute | solution.py:265
  11.9 4.3 %collective-permute-done.1.after_ref = f32[16,16,384]{2,1,0:T(8,128)S(1)} collective-permute-done((f32[16,16,384]{2,1,0:T(8,128)}, f32[16,16,384]{2,1,0:T(8,128)S(1)}, u32[]{:S(2)}, u32[]{:S(2)}) %collective-permute-start.1) | collective-permute-done | bytes 393248 | tf_op jit(solution)/shard_map/ppermute | solution.py:265
  16.2 0.8 %copy-done.1 = f32[16,16,384]{2,1,0:T(8,128)} copy-done((f32[16,16,384]{2,1,0:T(8,128)}, f32[16,16,384]{2,1,0:T(8,128)S(1)}, u32[]{:S(2)}) %copy-start.1) | copy-done | bytes 393240
  17.0 2.1 %strip.1 = f32[16,512]{1,0:T(8,128)} custom-call(f32[3,8,16,384]{3,2,1,0:T(8,128)} %get-tuple-element.18.own_ref, f32[16,16,384]{2,1,0:T(8,128)} %copy-done, f32[16,16,384]{2,1,0:T(8,128)} %copy-done.1), custom_call_target="tpu_custom_call" | custom-call | tf_op jit(solution)/shard_map/strip/pallas_call | solution.py:16
  19.1 1.3 %collective-permute-start.2 = (f32[16,512]{1,0:T(8,128)}, f32[16,512]{1,0:T(8,128)S(1)}, u32[]{:S(2)}, u32[]{:S(2)}) collective-permute-start(f32[16,512]{1,0:T(8,128)} %strip.1), channel_id=1, source_target_pairs={{0,1},{1,2},{2,3},{3,0},{4,5},{5,6},{6,7},{7,4},{8,9},{9,10},{10,1... | collective-permute-start | bytes 98312 | tf_op jit(solution)/shard_map/ppermute | solution.py:264
  20.4 1.3 %collective-permute-start.4 = (f32[384,128]{1,0:T(8,128)S(1)}, f32[384,128]{1,0:T(8,128)S(1)}, u32[]{:S(2)}, u32[]{:S(2)}) collective-permute-start(f32[384,128]{1,0:T(8,128)S(1)} %bitcast.35), channel_id=1, source_target_pairs={{16,0},{17,1},{18,2},{19,3},{20,4},{21,5},{22,6},{23,7},{24,8},{25... | collective-permute-start | bytes 589832 | tf_op jit(solution)/shard_map/ppermute | solution.py:265
  21.7 0.7 %copy.10.obs_ref = f32[16,1]{1,0:T(8,128)} copy(f32[16,1]{0,1:T(1,128)S(1)} %bitcast.36) | data formatting | bytes 128 | tf_op jit(solution)/shard_map/broadcast_in_dim | solution.py:290
  22.4 1.6 %collective-permute-done.2.strip_ref = f32[16,512]{1,0:T(8,128)S(1)} collective-permute-done((f32[16,512]{1,0:T(8,128)}, f32[16,512]{1,0:T(8,128)S(1)}, u32[]{:S(2)}, u32[]{:S(2)}) %collective-permute-start.2) | collective-permute-done | bytes 32800 | tf_op jit(solution)/shard_map/ppermute | solution.py:264
  24.5 4.7 %forward.1 = (f32[20,16,512]{2,1,0:T(8,128)}, f32[20,16,512]{2,1,0:T(8,128)}, f32[20,16,512]{2,1,0:T(8,128)}, f32[6,8,16,384]{3,2,1,0:T(8,128)}, f32[8,16,384]{2,1,0:T(8,128)}, /*index=5*/f32[8,16,384]{2,1,0:T(8,128)}) custom-call(s32[1]{0:T(128)} %bitcast.position_ref, s32[6]{0:T(128)} %taps_ref.3, f32[6]{0:T(128)} %weights_ref.3, f32[16,1]{1,0:T(8,128)} %copy.10.obs_ref, ...), custom_call_target="tpu_custom_call" | custom-call | tf_op jit(solution)/shard_map/forward/pallas_call | solution.py:16
  29.3 1.2 %collective-permute-start.3 = (f32[8,16,384]{2,1,0:T(8,128)}, f32[8,16,384]{2,1,0:T(8,128)S(1)}, u32[]{:S(2)}, u32[]{:S(2)}) collective-permute-start(f32[8,16,384]{2,1,0:T(8,128)} %get-tuple-element.25.filt_ref), channel_id=1, source_target_pairs={{0,16},{16,0},{1,17},{17,1},{2,18},{18,2},{3,19},{19,3},{4,20},{20... | collective-permute-start | bytes 589832 | tf_op jit(solution)/shard_map/ppermute | solution.py:277
  31.9 2.1 %collective-permute-done.3.other_ref = f32[8,16,384]{2,1,0:T(8,128)S(1)} collective-permute-done((f32[8,16,384]{2,1,0:T(8,128)}, f32[8,16,384]{2,1,0:T(8,128)S(1)}, u32[]{:S(2)}, u32[]{:S(2)}) %collective-permute-start.3) | collective-permute-done | bytes 196640 | tf_op jit(solution)/shard_map/ppermute | solution.py:277
  34.0 0.7 %copy-done.4 = f32[8,16,384]{2,1,0:T(8,128)} copy-done((f32[8,16,384]{2,1,0:T(8,128)}, f32[8,16,384]{2,1,0:T(8,128)S(1)}, u32[]{:S(2)}) %copy-start.4) | copy-done | bytes 196632
  34.7 4.2 %adjoint.1 = (f32[20,16,384]{2,1,0:T(8,128)}, f32[16,256]{1,0:T(8,128)}) custom-call(s32[1]{0:T(128)} %bitcast.position_ref, s32[6]{0:T(128)} %taps_ref.3, f32[6]{0:T(128)} %weights_ref.3, f32[16,1]{1,0:T(8,128)} %copy.13.err_ref, f32[16,1]{1,0:T(8,128)} %copy.12.pen_ref, f32[20,16,512]{2,1,0:T(8,128)} %get-tuple-element.21.adv_ref, ...), custom_call_target="tpu_custom_call" | custom-call | tf_op jit(solution)/shard_map/adjoint/pallas_call | solution.py:16
  38.9 1.5 %collective-permute-start.5 = (f32[16,256]{1,0:T(8,128)}, f32[16,256]{1,0:T(8,128)S(1)}, u32[]{:S(2)}, u32[]{:S(2)}) collective-permute-start(f32[16,256]{1,0:T(8,128)} %get-tuple-element.28), channel_id=1, source_target_pairs={{0,3},{1,0},{2,1},{3,2},{4,7},{5,4},{6,5},{7,6},{8,11},{9,8},{10,9... | collective-permute-start | bytes 49160 | tf_op jit(solution)/shard_map/ppermute | solution.py:264
  40.4 3.1 %collective-permute-start.8 = (f32[8,16,384]{2,1,0:T(8,128)S(1)}, f32[8,16,384]{2,1,0:T(8,128)S(1)}, u32[]{:S(2)}, u32[]{:S(2)}) collective-permute-start(f32[8,16,384]{2,1,0:T(8,128)S(1)} %copy-done.2), channel_id=1, source_target_pairs={{0,16},{1,17},{2,18},{3,19},{4,20},{5,21},{6,22},{7,23},{8,24},{9,... | collective-permute-start | bytes 589832 | tf_op jit(solution)/shard_map/ppermute | solution.py:265
  44.2 1.8 %spill.1 = (f32[6,16,384]{2,1,0:T(8,128)}, f32[6,16,384]{2,1,0:T(8,128)}) custom-call(f32[20,16,384]{2,1,0:T(8,128)} %get-tuple-element.27.main_ref, f32[16,256]{1,0:T(8,128)} %copy-done.9), custom_call_target="tpu_custom_call" | custom-call | tf_op jit(solution)/shard_map/spill/pallas_call | solution.py:16
  46.0 4.7 %collective-permute-start.6 = (f32[6,16,384]{2,1,0:T(8,128)}, f32[6,16,384]{2,1,0:T(8,128)S(1)}, u32[]{:S(2)}, u32[]{:S(2)}) collective-permute-start(f32[6,16,384]{2,1,0:T(8,128)} %get-tuple-element.29), channel_id=1, source_target_pairs={{0,4},{4,8},{8,12},{1,5},{5,9},{9,13},{2,6},{6,10},{10,14},{3,7},{... | collective-permute-start | bytes 442376 | tf_op jit(solution)/shard_map/ppermute | solution.py:265
  50.7 1.9 %collective-permute-start.7 = (f32[6,16,384]{2,1,0:T(8,128)}, f32[6,16,384]{2,1,0:T(8,128)S(1)}, u32[]{:S(2)}, u32[]{:S(2)}) collective-permute-start(f32[6,16,384]{2,1,0:T(8,128)} %get-tuple-element.30), channel_id=1, source_target_pairs={{4,0},{8,4},{12,8},{5,1},{9,5},{13,9},{6,2},{10,6},{14,10},{7,3},{... | collective-permute-start | bytes 442376 | tf_op jit(solution)/shard_map/ppermute | solution.py:265
  52.6 1.6 %slice_bitcast_fusion.x_ref = f32[8,16,384]{2,1,0:T(8,128)} fusion(f32[3,8,16,384]{3,2,1,0:T(8,128)} %get-tuple-element.18.own_ref), kind=kLoop, calls=%fused_computation | loop fusion | bytes 393216 | tf_op jit(solution)/shard_map/squeeze | solution.py:338
  54.3 3.1 %collective-permute-done.7.after_ref = f32[6,16,384]{2,1,0:T(8,128)S(1)} collective-permute-done((f32[6,16,384]{2,1,0:T(8,128)}, f32[6,16,384]{2,1,0:T(8,128)S(1)}, u32[]{:S(2)}, u32[]{:S(2)}) %collective-permute-start.7) | collective-permute-done | bytes 147488 | tf_op jit(solution)/shard_map/ppermute | solution.py:265
  58.0 2.1 %final.1 = f32[384,128]{1,0:T(8,128)} custom-call(s32[1]{0:T(128)} %bitcast.position_ref, f32[16,1]{1,0:T(8,128)} %copy.13.err_ref, f32[20,16,384]{2,1,0:T(8,128)} %get-tuple-element.27.main_ref, f32[16,256]{1,0:T(8,128)} %copy-done.9, f32[6,16,384]{2,1,0:T(8,128)} %copy-done.7, f32[6,16,384]{2,1,0:T(8,128)} %copy-done.8, ...), custom_call_target="tpu_custom_call" | custom-call | tf_op jit(solution)/shard_map/final/pallas_call | solution.py:16
  (32 shorter events, 3.2 us)
Async XLA Ops:
  0.0 20.4 %copy-start.6 = (f32[1,16,8,384]{3,2,1,0:T(8,128)S(1)}, f32[1,16,8,384]{3,2,1,0:T(8,128)}, u32[]{:S(2)}) copy-start(f32[1,16,8,384]{3,2,1,0:T(8,128)} %param.9) | copy-start | bytes 589828
  0.0 21.7 %copy-start.11 = (f32[16]{0:T(128)S(1)}, f32[16]{0:T(128)}, u32[]{:S(2)}) copy-start(f32[16]{0:T(128)} %param.13) | copy-start | bytes 196
  2.4 9.5 %collective-permute-start = (f32[16,16,384]{2,1,0:T(8,128)}, f32[16,16,384]{2,1,0:T(8,128)S(1)}, u32[]{:S(2)}, u32[]{:S(2)}) collective-permute-start(f32[16,16,384]{2,1,0:T(8,128)} %get-tuple-element.19), channel_id=1, source_target_pairs={{0,4},{4,8},{8,12},{1,5},{5,9},{9,13},{2,6},{6,10},{10,14},{3,7},{... | collective-permute-start | bytes 1179656 | tf_op jit(solution)/shard_map/ppermute | solution.py:265
  6.9 9.3 %collective-permute-start.1 = (f32[16,16,384]{2,1,0:T(8,128)}, f32[16,16,384]{2,1,0:T(8,128)S(1)}, u32[]{:S(2)}, u32[]{:S(2)}) collective-permute-start(f32[16,16,384]{2,1,0:T(8,128)} %get-tuple-element.20), channel_id=1, source_target_pairs={{4,0},{8,4},{12,8},{5,1},{9,5},{13,9},{6,2},{10,6},{14,10},{7,3},{... | collective-permute-start | bytes 1179656 | tf_op jit(solution)/shard_map/ppermute | solution.py:265
  11.9 4.3 %copy-start = (f32[16,16,384]{2,1,0:T(8,128)}, f32[16,16,384]{2,1,0:T(8,128)S(1)}, u32[]{:S(2)}) copy-start(f32[16,16,384]{2,1,0:T(8,128)S(1)} %collective-permute-done.before_ref) | copy-start | bytes 1179652
  16.2 0.8 %copy-start.1 = (f32[16,16,384]{2,1,0:T(8,128)}, f32[16,16,384]{2,1,0:T(8,128)S(1)}, u32[]{:S(2)}) copy-start(f32[16,16,384]{2,1,0:T(8,128)S(1)} %collective-permute-done.1.after_ref) | copy-start | bytes 1179652
  19.1 4.8 %collective-permute-start.2 = (f32[16,512]{1,0:T(8,128)}, f32[16,512]{1,0:T(8,128)S(1)}, u32[]{:S(2)}, u32[]{:S(2)}) collective-permute-start(f32[16,512]{1,0:T(8,128)} %strip.1), channel_id=1, source_target_pairs={{0,1},{1,2},{2,3},{3,0},{4,5},{5,6},{6,7},{7,4},{8,9},{9,10},{10,1... | collective-permute-start | bytes 98312 | tf_op jit(solution)/shard_map/ppermute | solution.py:264
  20.4 11.5 %collective-permute-start.4 = (f32[384,128]{1,0:T(8,128)S(1)}, f32[384,128]{1,0:T(8,128)S(1)}, u32[]{:S(2)}, u32[]{:S(2)}) collective-permute-start(f32[384,128]{1,0:T(8,128)S(1)} %bitcast.35), channel_id=1, source_target_pairs={{16,0},{17,1},{18,2},{19,3},{20,4},{21,5},{22,6},{23,7},{24,8},{25... | collective-permute-start | bytes 589832 | tf_op jit(solution)/shard_map/ppermute | solution.py:265
  23.9 0.6 copy-start.10
  24.5 6.0 %copy-start.12 = (f32[16]{0:T(128)S(1)}, f32[16]{0:T(128)}, u32[]{:S(2)}) copy-start(f32[16]{0:T(128)} %param.14) | copy-start | bytes 196
  24.5 6.7 %copy-start.13 = (f32[16]{0:T(128)S(1)}, f32[16]{0:T(128)}, u32[]{:S(2)}) copy-start(f32[16]{0:T(128)} %param.15) | copy-start | bytes 196
  29.3 4.7 %collective-permute-start.3 = (f32[8,16,384]{2,1,0:T(8,128)}, f32[8,16,384]{2,1,0:T(8,128)S(1)}, u32[]{:S(2)}, u32[]{:S(2)}) collective-permute-start(f32[8,16,384]{2,1,0:T(8,128)} %get-tuple-element.25.filt_ref), channel_id=1, source_target_pairs={{0,16},{16,0},{1,17},{17,1},{2,18},{18,2},{3,19},{19,3},{4,20},{20... | collective-permute-start | bytes 589832 | tf_op jit(solution)/shard_map/ppermute | solution.py:277
  31.9 2.1 %copy-start.3 = (f32[384,128]{1,0:T(8,128)}, f32[384,128]{1,0:T(8,128)S(1)}, u32[]{:S(2)}) copy-start(f32[384,128]{1,0:T(8,128)S(1)} %collective-permute-done.4.next_ref) | copy-start | bytes 589828
  34.0 0.7 %copy-start.4 = (f32[8,16,384]{2,1,0:T(8,128)}, f32[8,16,384]{2,1,0:T(8,128)S(1)}, u32[]{:S(2)}) copy-start(f32[8,16,384]{2,1,0:T(8,128)S(1)} %collective-permute-done.3.other_ref) | copy-start | bytes 589828
  34.7 5.7 %copy-start.2 = (f32[8,16,384]{2,1,0:T(8,128)S(1)}, f32[8,16,384]{2,1,0:T(8,128)}, u32[]{:S(2)}) copy-start(f32[8,16,384]{2,1,0:T(8,128)} %get-tuple-element.26.final_ref) | copy-start | bytes 589828
  38.9 4.6 %collective-permute-start.5 = (f32[16,256]{1,0:T(8,128)}, f32[16,256]{1,0:T(8,128)S(1)}, u32[]{:S(2)}, u32[]{:S(2)}) collective-permute-start(f32[16,256]{1,0:T(8,128)} %get-tuple-element.28), channel_id=1, source_target_pairs={{0,3},{1,0},{2,1},{3,2},{4,7},{5,4},{6,5},{7,6},{8,11},{9,8},{10,9... | collective-permute-start | bytes 49160 | tf_op jit(solution)/shard_map/ppermute | solution.py:264
  40.4 13.8 %collective-permute-start.8 = (f32[8,16,384]{2,1,0:T(8,128)S(1)}, f32[8,16,384]{2,1,0:T(8,128)S(1)}, u32[]{:S(2)}, u32[]{:S(2)}) collective-permute-start(f32[8,16,384]{2,1,0:T(8,128)S(1)} %copy-done.2), channel_id=1, source_target_pairs={{0,16},{1,17},{2,18},{3,19},{4,20},{5,21},{6,22},{7,23},{8,24},{9,... | collective-permute-start | bytes 589832 | tf_op jit(solution)/shard_map/ppermute | solution.py:265
  43.6 0.6 copy-start.9
  46.0 8.3 %collective-permute-start.6 = (f32[6,16,384]{2,1,0:T(8,128)}, f32[6,16,384]{2,1,0:T(8,128)S(1)}, u32[]{:S(2)}, u32[]{:S(2)}) collective-permute-start(f32[6,16,384]{2,1,0:T(8,128)} %get-tuple-element.29), channel_id=1, source_target_pairs={{0,4},{4,8},{8,12},{1,5},{5,9},{9,13},{2,6},{6,10},{10,14},{3,7},{... | collective-permute-start | bytes 442376 | tf_op jit(solution)/shard_map/ppermute | solution.py:265
  50.7 6.7 %collective-permute-start.7 = (f32[6,16,384]{2,1,0:T(8,128)}, f32[6,16,384]{2,1,0:T(8,128)S(1)}, u32[]{:S(2)}, u32[]{:S(2)}) collective-permute-start(f32[6,16,384]{2,1,0:T(8,128)} %get-tuple-element.30), channel_id=1, source_target_pairs={{4,0},{8,4},{12,8},{5,1},{9,5},{13,9},{6,2},{10,6},{14,10},{7,3},{... | collective-permute-start | bytes 442376 | tf_op jit(solution)/shard_map/ppermute | solution.py:265
  54.2 3.1 %copy-start.5 = (f32[8,16,384]{2,1,0:T(8,128)}, f32[8,16,384]{2,1,0:T(8,128)S(1)}, u32[]{:S(2)}) copy-start(f32[8,16,384]{2,1,0:T(8,128)S(1)} %collective-permute-done.8.previous_ref) | copy-start | bytes 589828
  54.2 3.1 %copy-start.7 = (f32[6,16,384]{2,1,0:T(8,128)}, f32[6,16,384]{2,1,0:T(8,128)S(1)}, u32[]{:S(2)}) copy-start(f32[6,16,384]{2,1,0:T(8,128)S(1)} %collective-permute-done.6.before_ref) | copy-start | bytes 442372
  57.4 0.7 %copy-start.8 = (f32[6,16,384]{2,1,0:T(8,128)}, f32[6,16,384]{2,1,0:T(8,128)S(1)}, u32[]{:S(2)}) copy-start(f32[6,16,384]{2,1,0:T(8,128)S(1)} %collective-permute-done.7.after_ref) | copy-start | bytes 442372

commit v2 on v1

--- a/solution.py
+++ b/solution.py
@@ -8,17 +8,24 @@
 
 LANES = 128
 F32 = jnp.float32
+SCOPED = 16 * 2**20
 VM = pl.BlockSpec(memory_space=pltpu.VMEM)
 SM = pl.BlockSpec(memory_space=pltpu.SMEM)
-
-
-def call(kernel, operands, specs, shapes, scratch=(), name=None):
+HB = pl.BlockSpec(memory_space=pltpu.HBM)
+
+
+def call(kernel, operands, specs, shapes, scratch=(), name=None, kept=True):
+    operands = [
+        pltpu.with_memory_space_constraint(o, pltpu.VMEM if spec is VM else pltpu.HBM) if spec is not SM else o
+        for o, spec in zip(operands, specs, strict=True)
+    ]
     return pl.pallas_call(
         kernel,
-        out_shape=[jax.ShapeDtypeStruct(s, F32) for s in shapes],
+        out_shape=[pltpu.VMEM(s, F32) if kept else jax.ShapeDtypeStruct(s, F32) for s in shapes],
         in_specs=specs,
         out_specs=[VM] * len(shapes),
         scratch_shapes=list(scratch),
+        compiler_params=pltpu.CompilerParams(vmem_limit_bytes=SCOPED),
         name=name,
     )(*operands)
 
@@ -78,29 +85,43 @@
     return jnp.swapaxes(split, 1, 2).reshape((levels, rows, cols))
 
 
-def pack_kernel(steps, rows, levels, x_ref, adv_ref, dif_ref, own_ref, up_ref, down_ref):
+def pack_kernel(
+    steps, rows, levels,
+    odd_ref, x_ref, adv_ref, dif_ref, own_ref, far_ref, near_ref, landing_ref, arrived,
+):
+    odd = jnp.full((levels, own_ref.shape[-1]), odd_ref[0]) == 1
     halos = (steps, steps - 1, steps - 1)
     base = 0
-    for field, ref in enumerate((x_ref, adv_ref, dif_ref)):
+    copies = [
+        pltpu.make_async_copy(ref, landing_ref.at[field], arrived.at[field])
+        for field, ref in enumerate((x_ref, adv_ref, dif_ref))
+    ]
+    for copy in copies:
+        copy.start()
+    for field, copy in enumerate(copies):
+        copy.wait()
+        ref = landing_ref.at[field]
         halo = halos[field]
+        values = [read_row(ref, levels, rows, r) for r in range(rows)]
         for r in range(rows):
-            value = read_row(ref, levels, rows, r)
-            own_ref[field, r] = value
-            if r < halo:
-                down_ref[base + r] = value
-            if r >= rows - halo:
-                up_ref[base + r - (rows - halo)] = value
+            own_ref[field, r] = values[r]
+        for q in range(halo):
+            down, up = values[q], values[rows - halo + q]
+            far_ref[base + q] = jnp.where(odd, up, down)
+            near_ref[base + q] = jnp.where(odd, down, up)
         base += halo
 
 
-def row_source(steps, rows, field, row, own_ref, before_ref, after_ref):
+def row_source(steps, rows, field, row, odd, own_ref, far_ref, near_ref):
     halo = (steps, steps - 1, steps - 1)[field]
     base = (0, steps, 2 * steps - 1)[field]
     if row < 0:
-        return before_ref, (base + row + halo,)
+        q = base + row + halo
+        return lambda cols: jnp.where(odd, near_ref[q, :, cols], far_ref[q, :, cols])
     if row >= rows:
-        return after_ref, (base + row - rows,)
-    return own_ref, (field, row)
+        q = base + row - rows
+        return lambda cols: jnp.where(odd, far_ref[q, :, cols], near_ref[q, :, cols])
+    return lambda cols: own_ref[field, row, :, cols]
 
 
 def wide_rows(steps, rows):
@@ -110,16 +131,26 @@
     return listed
 
 
-def strip_kernel(steps, rows, levels, own_ref, before_ref, after_ref, out_ref):
+def strip_kernel(steps, rows, levels, odd_ref, own_ref, far_ref, near_ref, out_ref):
+    odd = jnp.full((levels, LANES), odd_ref[0]) == 1
+
     def tile(field, row):
-        ref, index = row_source(steps, rows, field, row, own_ref, before_ref, after_ref)
-        return lambda: ref[index + (slice(None), slice(-LANES, None))]
+        read = row_source(steps, rows, field, row, odd, own_ref, far_ref, near_ref)
+        return lambda: read(slice(-LANES, None))
 
     packed = pack_slots(
         [tile(f, r) for f, r in wide_rows(steps, rows)], levels, steps, LANES - steps
     )
     for i, value in enumerate(packed):
         out_ref[:, i * LANES : (i + 1) * LANES] = value
+
+
+def per_level(ref, levels, cols):
+    level = lax.broadcasted_iota(jnp.int32, (levels, cols), 0)
+    value = jnp.zeros((levels, cols), F32)
+    for i in range(levels):
+        value = jnp.where(level == i, ref[i], value)
+    return value
 
 
 def coefficients(position, middle, steps, taps_ref, weights_ref):
@@ -135,20 +166,21 @@
 
 def forward_kernel(
     steps, rows, levels, middle,
-    position_ref, taps_ref, weights_ref, obs_ref, own_ref, before_ref, after_ref, strip_ref, dep_ref,
+    position_ref, odd_ref, taps_ref, weights_ref, obs_ref, own_ref, far_ref, near_ref, strip_ref, dep_ref,
     adv_ref, dif_ref, keep_ref, forcing_ref, filt_ref, final_ref,
     a_ref, b_ref,
 ):
     cols = own_ref.shape[-1]
     wide = cols + LANES
     coef = coefficients(position_ref[0], middle, steps, taps_ref, weights_ref)
-    obs = jnp.broadcast_to(obs_ref[...], (levels, cols))
+    obs = per_level(obs_ref, levels, cols)
+    odd = jnp.full((levels, cols), odd_ref[0]) == 1
     targets = (a_ref, adv_ref, dif_ref)
     for index, (field, row) in enumerate(wide_rows(steps, rows)):
-        ref, where = row_source(steps, rows, field, row, own_ref, before_ref, after_ref)
+        read = row_source(steps, rows, field, row, odd, own_ref, far_ref, near_ref)
         target = targets[field]
         target[row + steps, :, :LANES] = unpack_slot(strip_ref, index, levels, steps, LANES - steps)
-        target[row + steps, :, LANES:] = ref[where]
+        target[row + steps, :, LANES:] = read(slice(None))
     for ref in (adv_ref, dif_ref):
         for row in (0, rows + 2 * steps - 1):
             ref[row] = jnp.zeros((levels, wide), F32)
@@ -187,8 +219,8 @@
     position = position_ref[0]
     coef = coefficients(position, middle, steps, taps_ref, weights_ref)
     linked = jnp.where(position == members - 1, 0.0, 1.0).astype(F32)
-    err = jnp.broadcast_to(err_ref[...], (levels, cols)) * linked
-    pen = jnp.broadcast_to(pen_ref[...], (levels, cols))
+    err = per_level(err_ref, levels, cols) * linked
+    pen = per_level(pen_ref, levels, cols)
     zero = jnp.zeros((levels, wide), F32)
     for row in range(total_rows):
         if row < steps or row >= rows + steps:
@@ -226,21 +258,28 @@
         strip_ref[:, i * LANES : (i + 1) * LANES] = value
 
 
-def spill_kernel(steps, rows, levels, main_ref, strip_ref, up_ref, down_ref):
-    for i in range(steps):
-        for ref, row in ((down_ref, i), (up_ref, rows + steps + i)):
-            ref[i, :, :-LANES] = main_ref[row, :, :-LANES]
-            ref[i, :, -LANES:] = main_ref[row, :, -LANES:] + unpack_slot(
-                strip_ref, row, levels, steps, LANES - steps
-            )
+def spill_kernel(steps, rows, levels, odd_ref, main_ref, strip_ref, far_ref, near_ref):
+    odd = jnp.full((levels, main_ref.shape[-1]), odd_ref[0]) == 1
+
+    def full(row):
+        spilled = unpack_slot(strip_ref, row, levels, steps, LANES - steps)
+        return jnp.concatenate(
+            [main_ref[row, :, :-LANES], main_ref[row, :, -LANES:] + spilled], axis=1
+        )
+
+    for q in range(steps):
+        down, up = full(q), full(rows + steps + q)
+        far_ref[q] = jnp.where(odd, up, down)
+        near_ref[q] = jnp.where(odd, down, up)
 
 
 def final_kernel(
     steps, rows, levels,
-    position_ref, err_ref, main_ref, strip_ref, before_ref, after_ref, x_ref, previous_ref, out_ref,
+    position_ref, odd_ref, err_ref, main_ref, strip_ref, far_ref, near_ref, own_ref, previous_ref, out_ref,
 ):
     cols = main_ref.shape[-1]
-    err = jnp.broadcast_to(err_ref[...], (levels, cols))
+    err = per_level(err_ref, levels, cols)
+    odd = jnp.full((levels, cols), odd_ref[0]) == 1
     scale = jnp.where(position_ref[0] == 0, jnp.ones_like(err), err)
     for r in range(rows):
         row = r + steps
@@ -249,10 +288,11 @@
             [main_ref[row, :, :-LANES], main_ref[row, :, -LANES:] + spilled], axis=1
         )
         if r < steps:
-            value = value + before_ref[r]
+            value = value + jnp.where(odd, near_ref[r], far_ref[r])
         if r >= rows - steps:
-            value = value + after_ref[r - (rows - steps)]
-        value = value + scale * (x_ref[r] - previous_ref[r])
+            q = r - (rows - steps)
+            value = value + jnp.where(odd, far_ref[q], near_ref[q])
+        value = value + scale * (own_ref[0, r] - previous_ref[r])
         tiles = cols // LANES
         for c in range(tiles):
             out_ref[pl.ds(c * rows + r, levels, stride=rows * tiles), :] = value[:, c * LANES : (c + 1) * LANES]
@@ -263,6 +303,13 @@
     if ring:
         return lax.ppermute(value, axis, [(i, (i + by) % count) for i in range(count)])
     return lax.ppermute(value, axis, [(i, i + by) for i in range(count) if 0 <= i + by < count])
+
+
+def exchanged(far, near, axis):
+    count = lax.axis_size(axis)
+    far = lax.ppermute(far, axis, [p for i in range(1, count - 1, 2) for p in ((i, i + 1), (i + 1, i))])
+    near = lax.ppermute(near, axis, [p for i in range(0, count - 1, 2) for p in ((i, i + 1), (i + 1, i))])
+    return far, near
 
 
 def halves(value, axis):
@@ -287,7 +334,7 @@
     _, steps, levels, rows, cols = departures.shape
     middle = members * steps // 2
     position = lax.axis_index("tm").astype(jnp.int32)[None]
-    obs, err, pen = (w[:, None] for w in (obs_weight, error_weight, penalty_weight))
+    odd = (lax.axis_index("lat").astype(jnp.int32) % 2)[None]
     x, adv, dif, dep = (tiled(v) for v in (increments, advection, diffusion, departures))
     bind = functools.partial
     total_rows = rows + 2 * steps
@@ -295,25 +342,25 @@
     halo_rows = 3 * steps - 2
     row_set = (levels, cols)
 
-    own, up, down = call(
-        bind(pack_kernel, steps, rows, levels), (x, adv, dif), [VM] * 3,
-        [(3, rows) + row_set, (halo_rows,) + row_set, (halo_rows,) + row_set], name="pack",
-    )
-    before = along(up, "lat", 1)
-    after = along(down, "lat", -1)
+    own, far, near = call(
+        bind(pack_kernel, steps, rows, levels), (odd, x, adv, dif), [SM] + [HB] * 3,
+        [(3, rows) + row_set, (halo_rows,) + row_set, (halo_rows,) + row_set],
+        [pltpu.VMEM((3,) + x.shape, F32), pltpu.SemaphoreType.DMA((3,))], name="pack",
+    )
+    far, near = exchanged(far, near, "lat")
     following = along(x, "tm", -1)
 
     strip_shape = (levels, LANES * lane_slots(len(wide_rows(steps, rows)), steps))
     (strip,) = call(
-        bind(strip_kernel, steps, rows, levels), (own, before, after), [VM] * 3, [strip_shape], name="strip",
+        bind(strip_kernel, steps, rows, levels), (odd, own, far, near), [SM] + [VM] * 3, [strip_shape], name="strip",
     )
     strip = along(strip, "lon", 1, ring=True)
 
     wide_shape = (total_rows, levels, wide)
     adv_w, dif_w, keep_w, forcing, filt, final = call(
         bind(forward_kernel, steps, rows, levels, middle),
-        (position, filter_steps, filter_weights, obs, own, before, after, strip, dep),
-        [SM] * 3 + [VM] * 6,
+        (position, odd, filter_steps, filter_weights, obs_weight, own, far, near, strip, dep),
+        [SM] * 5 + [VM] * 5,
         [wide_shape] * 3 + [(steps, rows) + row_set, (rows,) + row_set, (rows,) + row_set],
         [pltpu.VMEM(wide_shape, F32)] * 2, name="forward",
     )
@@ -322,20 +369,19 @@
 
     main, spill = call(
         bind(adjoint_kernel, steps, rows, levels, middle, members),
-        (position, filter_steps, filter_weights, err, pen, adv_w, dif_w, keep_w, forcing, filt, other, final, following),
-        [SM] * 3 + [VM] * 10,
+        (position, filter_steps, filter_weights, error_weight, penalty_weight, adv_w, dif_w, keep_w, forcing, filt, other, final, following),
+        [SM] * 5 + [VM] * 8,
         [(total_rows,) + row_set, (levels, LANES * lane_slots(total_rows, steps))],
         [pltpu.VMEM(wide_shape, F32)] * 2 + [pltpu.VMEM((rows,) + row_set, F32)], name="adjoint",
     )
     spill = along(spill, "lon", -1, ring=True)
-    up, down = call(
-        bind(spill_kernel, steps, rows, levels), (main, spill), [VM] * 2, [(steps,) + row_set] * 2, name="spill",
-    )
-    before = along(up, "lat", 1)
-    after = along(down, "lat", -1)
+    far, near = call(
+        bind(spill_kernel, steps, rows, levels), (odd, main, spill), [SM] + [VM] * 2, [(steps,) + row_set] * 2, name="spill",
+    )
+    far, near = exchanged(far, near, "lat")
     (out,) = call(
         bind(final_kernel, steps, rows, levels),
-        (position, err, main, spill, before, after, own[0], previous), [SM] + [VM] * 7, [x.shape], name="final",
+        (position, odd, error_weight, main, spill, far, near, own, previous), [SM] * 3 + [VM] * 6, [x.shape], name="final", kept=False,
     )
     return untiled(out, levels, rows, cols)[None]
 

time: 60.5 us -> 39.1 us (0.65)
  Pallas kernels: 17.4 us -> 7.07 us
  local copies, waits for them, and re-layouts: 6.98 us -> 0.03 us
  starting transfers between devices: 21.4 us -> 17.9 us
    ppermute x6 -> x2, starting transfers between devices: 17.4 us -> 3.41 us  [along(): lax.ppermute(value, axis, [(i, i + by) for i in range(count) if 0 <= i +...]
    ppermute x6 -> x2, waiting for transfers between devices: 10.5 us -> 0.01 us  [along(): lax.ppermute(value, axis, [(i, i + by) for i in range(count) if 0 <= i +...]
    pallas_call x6, Pallas kernels: 17.4 us -> 7.07 us  [call(): pl.pallas_call(kernel, out_shape=[pltpu.VMEM(s, F32) if kept else jax.Sha...]
    ppermute x0 -> x4, starting transfers between devices: none -> 10.2 us  [the longest x2 10 us: exchanged(): lax.ppermute(far, axis, [p for i in range(1, count - 1, 2) for p in ((i,...]
    ppermute x0 -> x4, waiting for transfers between devices: none -> 8.09 us  [the longest x2 8.09 us: exchanged(): lax.ppermute(far, axis, [p for i in range(1, count - 1, 2) for p in ((i,...]
    unnamed x28 -> x14, local copies, waits for them, and re-layouts: 3.35 us -> 0.03 us
    broadcast_in_dim x3 -> x0, local copies, waits for them, and re-layouts: 2.02 us -> none  [body(): w[:, None]]
    ppermute x2, waiting for transfers between devices: 1.56 us -> 3.23 us  [along(): lax.ppermute(value, axis, [(i, (i + by) % count) for i in range(count)])]
  transfers between devices with their start and end apart: 9 -> 9, of which waited for: 5 -> 5; matrix products, arithmetic and copies ran while one was open for 6% -> 0% of each run, Pallas kernels for 11% -> 11%
where the time goes in v2:
time: 39.1 us; the launch traced here: 38.9 us
  starting transfers between devices  17.9 us (46%)
  waiting for transfers between devices  13.7 us (35%)
  Pallas kernels  7.07 us (18%)
    ppermute x2, starting transfers between devices, exchanged(): lax.ppermute(far, axis, [p for i in range(1, count - 1, 2) for p in ((i,...  10 us
    ppermute x2, waiting for transfers between devices, exchanged(): lax.ppermute(far, axis, [p for i in range(1, count - 1, 2) for p in ((i,...  8.09 us
    pallas_call x6, Pallas kernels, call(): pl.pallas_call(kernel, out_shape=[pltpu.VMEM(s, F32) if kept else jax.Sha...  7.07 us
    ppermute x2, starting transfers between devices, along(): lax.ppermute(value, axis, [(i, i + by) for i in range(count) if 0 <= i +...  3.41 us
    ppermute x2, waiting for transfers between devices, along(): lax.ppermute(value, axis, [(i, (i + by) % count) for i in range(count)])  3.23 us
    ppermute x2, starting transfers between devices, along(): lax.ppermute(value, axis, [(i, (i + by) % count) for i in range(count)])  3.03 us
    ppermute x1, waiting for transfers between devices, halves(): other = lax.ppermute(value, axis, [(i, i ^ distance) for i in range(count)])  2.4 us
    ppermute x1, starting transfers between devices, halves(): other = lax.ppermute(value, axis, [(i, i ^ distance) for i in range(count)])  1.3 us
  transfers between devices with their start and end apart: 9, of which 5 were waited for; matrix products, arithmetic and copies ran while one was open for 0% of the time, Pallas kernels for 11%

profile of v2, /device:TPU:1, one launch (start us, length us, event | category | flops | bytes accessed | tf_op | source)
XLA Modules:
  0.0 38.9 jit_solution(400794627332561246)
XLA Ops:
  0.0 1.3 %pack.1 = (f32[3,8,16,384]{3,2,1,0:T(8,128)S(1)}, f32[16,16,384]{2,1,0:T(8,128)S(1)}, f32[16,16,384]{2,1,0:T(8,128)S(1)}) custom-call(s32[1]{0:T(128)} %bitcast.1.odd_ref, f32[384,128]{1,0:T(8,128)} %bitcast.30, f32[384,128]{1,0:T(8,128)} %bitcast.28, f32[384,128]{1,0:T(8,128)} %bitcast.29), custom_call_target="tpu_custom_call" | custom-call | tf_op jit(solution)/shard_map/pack/pallas_call | solution.py:22
  1.3 4.5 %collective-permute-start = (f32[16,16,384]{2,1,0:T(8,128)S(1)}, f32[16,16,384]{2,1,0:T(8,128)S(1)}, u32[]{:S(2)}, u32[]{:S(2)}) collective-permute-start(f32[16,16,384]{2,1,0:T(8,128)S(1)} %get-tuple-element.19), channel_id=1, source_target_pairs={{4,8},{8,4},{5,9},{9,5},{6,10},{10,6},{7,11},{11,7},{20,24},{24,20... | collective-permute-start | bytes 1179656 | tf_op jit(solution)/shard_map/ppermute | solution.py:310
  5.8 0.1 collective-permute-start.1
  5.9 5.4 %collective-permute-done.far_ref = f32[16,16,384]{2,1,0:T(8,128)S(1)} collective-permute-done((f32[16,16,384]{2,1,0:T(8,128)S(1)}, f32[16,16,384]{2,1,0:T(8,128)S(1)}, u32[]{:S(2)}, u32[]{:S(2)}) %collective-permute-start) | collective-permute-done | bytes 393248 | tf_op jit(solution)/shard_map/ppermute | solution.py:310
  11.3 0.2 strip.1
  11.5 1.6 %collective-permute-start.2 = (f32[16,512]{1,0:T(8,128)S(1)}, f32[16,512]{1,0:T(8,128)S(1)}, u32[]{:S(2)}, u32[]{:S(2)}) collective-permute-start(f32[16,512]{1,0:T(8,128)S(1)} %strip.1), channel_id=1, source_target_pairs={{0,1},{1,2},{2,3},{3,0},{4,5},{5,6},{6,7},{7,4},{8,9},{9,10},{10,1... | collective-permute-start | bytes 98312 | tf_op jit(solution)/shard_map/ppermute | solution.py:304
  13.1 1.3 %collective-permute-start.4 = (f32[384,128]{1,0:T(8,128)S(1)}, f32[384,128]{1,0:T(8,128)S(1)}, u32[]{:S(2)}, u32[]{:S(2)}) collective-permute-start(f32[384,128]{1,0:T(8,128)S(1)} %bitcast.31), channel_id=1, source_target_pairs={{16,0},{17,1},{18,2},{19,3},{20,4},{21,5},{22,6},{23,7},{24,8},{25... | collective-permute-start | bytes 589832 | tf_op jit(solution)/shard_map/ppermute | solution.py:305
  14.4 2.0 %collective-permute-done.2.strip_ref = f32[16,512]{1,0:T(8,128)S(1)} collective-permute-done((f32[16,512]{1,0:T(8,128)S(1)}, f32[16,512]{1,0:T(8,128)S(1)}, u32[]{:S(2)}, u32[]{:S(2)}) %collective-permute-start.2) | collective-permute-done | bytes 32800 | tf_op jit(solution)/shard_map/ppermute | solution.py:304
  16.4 0.0 copy-start.3
  16.4 0.0 copy-start.5
  16.4 2.2 %forward.1 = (f32[20,16,512]{2,1,0:T(8,128)S(1)}, f32[20,16,512]{2,1,0:T(8,128)S(1)}, f32[20,16,512]{2,1,0:T(8,128)S(1)}, f32[6,8,16,384]{3,2,1,0:T(8,128)S(1)},...) custom-call(s32[1]{0:T(128)} %bitcast.position_ref, s32[1]{0:T(128)} %bitcast.1.odd_ref, s32[6]{0:T(128)S(1)} %copy-done.1, ...), custom_call_target="tpu_custom_call" | custom-call | tf_op jit(solution)/shard_map/forward/pallas_call | solution.py:22
  18.6 1.3 %collective-permute-start.3 = (f32[8,16,384]{2,1,0:T(8,128)S(1)}, f32[8,16,384]{2,1,0:T(8,128)S(1)}, u32[]{:S(2)}, u32[]{:S(2)}) collective-permute-start(f32[8,16,384]{2,1,0:T(8,128)S(1)} %get-tuple-element.25.filt_ref), channel_id=1, source_target_pairs={{0,16},{16,0},{1,17},{17,1},{2,18},{18,2},{3,19},{19,3},{4,20},{20... | collective-permute-start | bytes 589832 | tf_op jit(solution)/shard_map/ppermute | solution.py:324
  19.9 2.1 %collective-permute-start.8 = (f32[8,16,384]{2,1,0:T(8,128)S(1)}, f32[8,16,384]{2,1,0:T(8,128)S(1)}, u32[]{:S(2)}, u32[]{:S(2)}) collective-permute-start(f32[8,16,384]{2,1,0:T(8,128)S(1)} %get-tuple-element.26.final_ref), channel_id=1, source_target_pairs={{0,16},{1,17},{2,18},{3,19},{4,20},{5,21},{6,22},{7,23},{8,24},{9,... | collective-permute-start | bytes 589832 | tf_op jit(solution)/shard_map/ppermute | solution.py:305
  22.0 2.4 %collective-permute-done.3.other_ref = f32[8,16,384]{2,1,0:T(8,128)S(1)} collective-permute-done((f32[8,16,384]{2,1,0:T(8,128)S(1)}, f32[8,16,384]{2,1,0:T(8,128)S(1)}, u32[]{:S(2)}, u32[]{:S(2)}) %collective-permute-start.3) | collective-permute-done | bytes 196640 | tf_op jit(solution)/shard_map/ppermute | solution.py:324
  24.5 2.0 %adjoint.1 = (f32[20,16,384]{2,1,0:T(8,128)S(1)}, f32[16,256]{1,0:T(8,128)S(1)}) custom-call(s32[1]{0:T(128)} %bitcast.position_ref, s32[6]{0:T(128)S(1)} %copy-done.1, f32[6]{0:T(128)S(1)} %copy-done.2, f32[16]{0:T(128)S(1)} %copy-done.3, f32[16]{0:T(128)S(1)} %copy-done.5, f32[20,16,512]{2,1,0:T(8,128)S(1)} %get-tuple-element.21.adv_ref, ...), custom_call_target="tpu_custom_call" | custom-call | tf_op jit(solution)/shard_map/adjoint/pallas_call | solution.py:22
  26.5 1.4 %collective-permute-start.5 = (f32[16,256]{1,0:T(8,128)S(1)}, f32[16,256]{1,0:T(8,128)S(1)}, u32[]{:S(2)}, u32[]{:S(2)}) collective-permute-start(f32[16,256]{1,0:T(8,128)S(1)} %get-tuple-element.28), channel_id=1, source_target_pairs={{0,3},{1,0},{2,1},{3,2},{4,7},{5,4},{6,5},{7,6},{8,11},{9,8},{10,9... | collective-permute-start | bytes 49160 | tf_op jit(solution)/shard_map/ppermute | solution.py:304
  27.9 1.2 %collective-permute-done.5.strip_ref = f32[16,256]{1,0:T(8,128)S(1)} collective-permute-done((f32[16,256]{1,0:T(8,128)S(1)}, f32[16,256]{1,0:T(8,128)S(1)}, u32[]{:S(2)}, u32[]{:S(2)}) %collective-permute-start.5) | collective-permute-done | bytes 16416 | tf_op jit(solution)/shard_map/ppermute | solution.py:304
  29.1 0.1 spill.1
  29.2 5.5 %collective-permute-start.6 = (f32[6,16,384]{2,1,0:T(8,128)S(1)}, f32[6,16,384]{2,1,0:T(8,128)S(1)}, u32[]{:S(2)}, u32[]{:S(2)}) collective-permute-start(f32[6,16,384]{2,1,0:T(8,128)S(1)} %get-tuple-element.29), channel_id=1, source_target_pairs={{4,8},{8,4},{5,9},{9,5},{6,10},{10,6},{7,11},{11,7},{20,24},{24,20... | collective-permute-start | bytes 442376 | tf_op jit(solution)/shard_map/ppermute | solution.py:310
  34.8 0.1 collective-permute-start.7
  34.9 0.0 collective-permute-done.8.previous_ref
  34.9 2.7 %collective-permute-done.6.far_ref = f32[6,16,384]{2,1,0:T(8,128)S(1)} collective-permute-done((f32[6,16,384]{2,1,0:T(8,128)S(1)}, f32[6,16,384]{2,1,0:T(8,128)S(1)}, u32[]{:S(2)}, u32[]{:S(2)}) %collective-permute-start.6) | collective-permute-done | bytes 147488 | tf_op jit(solution)/shard_map/ppermute | solution.py:310
  37.6 0.0 collective-permute-done.7.near_ref
  37.6 1.3 %final.1 = f32[384,128]{1,0:T(8,128)} custom-call(s32[1]{0:T(128)} %bitcast.position_ref, s32[1]{0:T(128)} %bitcast.1.odd_ref, f32[16]{0:T(128)S(1)} %copy-done.3, f32[20,16,384]{2,1,0:T(8,128)S(1)} %get-tuple-element.27.main_ref, f32[16,256]{1,0:T(8,128)S(1)} %collective-permute-done.5.strip_ref, f32[6,16,384]{2,1,0:T(8,128)S(1)} %collective-permute-done.6.far_ref, ...), custom_call_target="tpu_custom_call" | custom-call | tf_op jit(solution)/shard_map/final/pallas_call | solution.py:22
  (14 shorter events, 0.0 us)
Async XLA Ops:
  0.0 13.1 %copy-start.6 = (f32[1,16,8,384]{3,2,1,0:T(8,128)S(1)}, f32[1,16,8,384]{3,2,1,0:T(8,128)}, u32[]{:S(2)}) copy-start(f32[1,16,8,384]{3,2,1,0:T(8,128)} %param.9) | copy-start | bytes 589828
  0.0 16.4 %copy-start = (f32[1,6,16,8,384]{4,3,2,1,0:T(8,128)S(1)}, f32[1,6,16,8,384]{4,3,2,1,0:T(8,128)}, u32[]{:S(2)}) copy-start(f32[1,6,16,8,384]{4,3,2,1,0:T(8,128)} %param.12) | copy-start | bytes 3538948
  0.0 16.4 %copy-start.4 = (f32[16]{0:T(128)S(1)}, f32[16]{0:T(128)}, u32[]{:S(2)}) copy-start(f32[16]{0:T(128)} %obs_ref.1) | copy-start | bytes 196
  0.0 16.4 %copy-start.1 = (s32[6]{0:T(128)S(1)}, s32[6]{0:T(128)}, u32[]{:S(2)}) copy-start(s32[6]{0:T(128)} %taps_ref.3) | copy-start | bytes 76
  0.0 16.4 %copy-start.2 = (f32[6]{0:T(128)S(1)}, f32[6]{0:T(128)}, u32[]{:S(2)}) copy-start(f32[6]{0:T(128)} %weights_ref.3) | copy-start | bytes 76
  1.3 10.0 %collective-permute-start = (f32[16,16,384]{2,1,0:T(8,128)S(1)}, f32[16,16,384]{2,1,0:T(8,128)S(1)}, u32[]{:S(2)}, u32[]{:S(2)}) collective-permute-start(f32[16,16,384]{2,1,0:T(8,128)S(1)} %get-tuple-element.19), channel_id=1, source_target_pairs={{4,8},{8,4},{5,9},{9,5},{6,10},{10,6},{7,11},{11,7},{20,24},{24,20... | collective-permute-start | bytes 1179656 | tf_op jit(solution)/shard_map/ppermute | solution.py:310
  5.8 5.4 %collective-permute-start.1 = (f32[16,16,384]{2,1,0:T(8,128)S(1)}, f32[16,16,384]{2,1,0:T(8,128)S(1)}, u32[]{:S(2)}, u32[]{:S(2)}) collective-permute-start(f32[16,16,384]{2,1,0:T(8,128)S(1)} %get-tuple-element.20), channel_id=1, source_target_pairs={{0,4},{4,0},{8,12},{12,8},{1,5},{5,1},{9,13},{13,9},{2,6},{6,2},{1... | collective-permute-start | bytes 1179656 | tf_op jit(solution)/shard_map/ppermute | solution.py:311
  11.5 4.9 %collective-permute-start.2 = (f32[16,512]{1,0:T(8,128)S(1)}, f32[16,512]{1,0:T(8,128)S(1)}, u32[]{:S(2)}, u32[]{:S(2)}) collective-permute-start(f32[16,512]{1,0:T(8,128)S(1)} %strip.1), channel_id=1, source_target_pairs={{0,1},{1,2},{2,3},{3,0},{4,5},{5,6},{6,7},{7,4},{8,9},{9,10},{10,1... | collective-permute-start | bytes 98312 | tf_op jit(solution)/shard_map/ppermute | solution.py:304
  13.1 9.0 %collective-permute-start.4 = (f32[384,128]{1,0:T(8,128)S(1)}, f32[384,128]{1,0:T(8,128)S(1)}, u32[]{:S(2)}, u32[]{:S(2)}) collective-permute-start(f32[384,128]{1,0:T(8,128)S(1)} %bitcast.31), channel_id=1, source_target_pairs={{16,0},{17,1},{18,2},{19,3},{20,4},{21,5},{22,6},{23,7},{24,8},{25... | collective-permute-start | bytes 589832 | tf_op jit(solution)/shard_map/ppermute | solution.py:305
  16.4 8.0 %copy-start.3 = (f32[16]{0:T(128)S(1)}, f32[16]{0:T(128)}, u32[]{:S(2)}) copy-start(f32[16]{0:T(128)} %err_ref.3) | copy-start | bytes 196
  16.4 8.0 %copy-start.5 = (f32[16]{0:T(128)S(1)}, f32[16]{0:T(128)}, u32[]{:S(2)}) copy-start(f32[16]{0:T(128)} %pen_ref.1) | copy-start | bytes 196
  18.6 5.9 %collective-permute-start.3 = (f32[8,16,384]{2,1,0:T(8,128)S(1)}, f32[8,16,384]{2,1,0:T(8,128)S(1)}, u32[]{:S(2)}, u32[]{:S(2)}) collective-permute-start(f32[8,16,384]{2,1,0:T(8,128)S(1)} %get-tuple-element.25.filt_ref), channel_id=1, source_target_pairs={{0,16},{16,0},{1,17},{17,1},{2,18},{18,2},{3,19},{19,3},{4,20},{20... | collective-permute-start | bytes 589832 | tf_op jit(solution)/shard_map/ppermute | solution.py:324
  19.9 15.0 %collective-permute-start.8 = (f32[8,16,384]{2,1,0:T(8,128)S(1)}, f32[8,16,384]{2,1,0:T(8,128)S(1)}, u32[]{:S(2)}, u32[]{:S(2)}) collective-permute-start(f32[8,16,384]{2,1,0:T(8,128)S(1)} %get-tuple-element.26.final_ref), channel_id=1, source_target_pairs={{0,16},{1,17},{2,18},{3,19},{4,20},{5,21},{6,22},{7,23},{8,24},{9,... | collective-permute-start | bytes 589832 | tf_op jit(solution)/shard_map/ppermute | solution.py:305
  26.5 2.6 %collective-permute-start.5 = (f32[16,256]{1,0:T(8,128)S(1)}, f32[16,256]{1,0:T(8,128)S(1)}, u32[]{:S(2)}, u32[]{:S(2)}) collective-permute-start(f32[16,256]{1,0:T(8,128)S(1)} %get-tuple-element.28), channel_id=1, source_target_pairs={{0,3},{1,0},{2,1},{3,2},{4,7},{5,4},{6,5},{7,6},{8,11},{9,8},{10,9... | collective-permute-start | bytes 49160 | tf_op jit(solution)/shard_map/ppermute | solution.py:304
  29.2 8.3 %collective-permute-start.6 = (f32[6,16,384]{2,1,0:T(8,128)S(1)}, f32[6,16,384]{2,1,0:T(8,128)S(1)}, u32[]{:S(2)}, u32[]{:S(2)}) collective-permute-start(f32[6,16,384]{2,1,0:T(8,128)S(1)} %get-tuple-element.29), channel_id=1, source_target_pairs={{4,8},{8,4},{5,9},{9,5},{6,10},{10,6},{7,11},{11,7},{20,24},{24,20... | collective-permute-start | bytes 442376 | tf_op jit(solution)/shard_map/ppermute | solution.py:310
  34.8 2.8 %collective-permute-start.7 = (f32[6,16,384]{2,1,0:T(8,128)S(1)}, f32[6,16,384]{2,1,0:T(8,128)S(1)}, u32[]{:S(2)}, u32[]{:S(2)}) collective-permute-start(f32[6,16,384]{2,1,0:T(8,128)S(1)} %get-tuple-element.30), channel_id=1, source_target_pairs={{0,4},{4,0},{8,12},{12,8},{1,5},{5,1},{9,13},{13,9},{2,6},{6,2},{1... | collective-permute-start | bytes 442376 | tf_op jit(solution)/shard_map/ppermute | solution.py:311
